TPU v7x, 128 devices: a whole 4x4x4 slice. The times are simulated.
128 devices in a mesh: dp: 8 (over y, core), expert: 16 (over z, x).
Axes of the slice: x: 4, y: 4, z: 4, core: 2. Of those that a mesh axis runs over, the one named last changes fastest.
Arguments:
- tokens: bfloat16 [8, 4, 8192, 1024], P('dp', None, 'expert'), may hold values from -8000 to 8000
- slot_params: bfloat16 [1024, 256], replicated, may hold values from -8 to 8
- dest: int32 [8, 4, 32], P('dp', None, 'expert'), may hold values from 0 to 127, as said below
- lengths: int32 [8, 4], P('dp'), may hold values from 256 to 8192
- w_in: bfloat16 [128, 1024, 4096], P('expert', None, 'dp'), may hold values from -0.1875 to 0.1875
- w_out: bfloat16 [128, 4096, 1024], P('expert', 'dp'), may hold values from -3 to 3
Outputs:
- mixed: bfloat16 [8, 128, 256, 1024], P('dp', 'expert')
Inputs may be any that keep to these rules, and one draw needn't show every extreme that they name: For each g, dest[g] holds every number of 0 to 127 once; the 8 blocks held by one device (block indices j from k * 2 on, for every q) go to output blocks of different devices, device d holding output blocks d * 4 * 2 onward, so each device receives at most one block from each device.
All inputs are finite; a program needn't handle non-finite values.
Results may differ from a plain program's by a relative error of at most 0.01.
Values may be sent and summed in bfloat16 or wider, within the bound.
No kernel may reach another device: no remote copies, remote signals or barrier semaphores. Data moves between devices by JAX's collectives and lax.ppermute only.
A program may use at most 128 MiB of HBM per device.

v0:
```python
import functools
import math

import jax
import jax.numpy as jnp
from jax import lax
from jax.experimental import pallas as pl
from jax.experimental.pallas import tpu as pltpu
from jax.sharding import Mesh
from jax.sharding import PartitionSpec as P


DP = ("y", "c")
EXPERT = ("z", "x")
LANES = 128
PIECES = 8
TAGS = 64
NO_TOKEN = -1e30
F32 = jnp.float32
BF16 = jnp.bfloat16


def pieces_of(value):
    high = value.astype(BF16).astype(F32)
    rest = value - high
    middle = rest.astype(BF16).astype(F32)
    return high, middle, rest - middle


def small(mebibytes):
    return pltpu.CompilerParams(vmem_limit_bytes=mebibytes * 1024 * 1024)


def in_vmem(*arrays):
    return [pltpu.with_memory_space_constraint(array, pltpu.VMEM) for array in arrays]


def in_hbm(*arrays):
    return [pltpu.with_memory_space_constraint(array, pltpu.HBM) for array in arrays]


ANYWHERE = pl.BlockSpec(memory_space=pl.ANY)
WHOLE = pl.BlockSpec(memory_space=pltpu.VMEM)
SCALARS = pl.BlockSpec(memory_space=pltpu.SMEM)


def line_order(total, owned, swap):
    side = math.isqrt(total // owned)
    column = lax.broadcasted_iota(jnp.int32, (total, total), 1)
    place = column // owned
    shard = jnp.where(swap, place % side * side + place // side, place)
    source = shard * owned + column % owned
    return (lax.broadcasted_iota(jnp.int32, (total, total), 0) == source).astype(BF16)


def dispatch_kernel(lengths, dest, place, tokens, params, *refs):
    side = 4
    parts = refs[:side]
    mixes, plain, order, held_tokens, sums, turned, stats, labels, blocks, loads, sems = refs[side:]
    shard, core, line = place[0], place[1], place[2]
    _, seqs, length, width = tokens.shape
    slots = params.shape[1]
    owned = slots // (side * side)
    slabs = width // LANES
    stat_rows = parts[0].shape[1] - owned
    block = mixes.shape[1]
    per_seq = length // block
    held = per_seq * seqs
    group = side * owned

    first_load = pltpu.make_async_copy(params, plain, loads.at[seqs])
    first_load.start()
    arrivals = []
    for q in range(seqs):
        arrivals.append(pltpu.make_async_copy(tokens.at[0, q], held_tokens.at[q], loads.at[q]))
        arrivals[-1].start()
    stats[...] = jnp.zeros(stats.shape, stats.dtype)
    for d in range(side * side):
        labels[d] = 0
    for j in range(per_seq):
        for q in range(seqs):
            target = dest[j, q]
            labels[lax.div(target, held)] = lax.rem(target, held) * seqs + q + 1
    sorting = line_order(slots, owned, core == 1)
    first_load.wait()
    order[...] = jnp.dot(plain[...], sorting, preferred_element_type=F32).astype(BF16)

    sends = []
    row = lax.broadcasted_iota(jnp.int32, (PIECES, slots), 0)
    for q in range(seqs):
        arrivals[q].wait()
        feats = held_tokens[q]
        logits = jnp.dot(feats, order[...], preferred_element_type=F32)
        count = lengths[0, q] - shard * length
        live = lax.broadcasted_iota(jnp.int32, (length, 1), 0) < count
        masked = jnp.where(live, logits, NO_TOKEN)
        top = jnp.max(masked, axis=0, keepdims=True)
        weight = jnp.where(live, jnp.exp(masked - top), 0.0)
        mass = jnp.sum(weight, axis=0, keepdims=True)
        sums[q] = lax.dot_general(
            weight.astype(BF16), feats, (((0,), (0,)), ((), ())), preferred_element_type=F32
        ).astype(BF16)
        for k, part in enumerate(parts):
            first = pl.multiple_of(lax.rem(line + k, side) * group, group)
            numer = sums[q, pl.ds(first, group), :]
            for j in range(slabs):
                start = (j * seqs + q) * owned
                piece = numer[:, j * LANES : (j + 1) * LANES]
                part[:, start : start + owned, :] = piece.reshape(side, owned, LANES)
        stacked = jnp.zeros((PIECES, slots), F32)
        for k, piece in enumerate(pieces_of(top) + pieces_of(mass)):
            stacked = jnp.where(row == k, piece, stacked)
        stats[q * PIECES : (q + 1) * PIECES, :] = stacked

        peak = jnp.max(logits, axis=1, keepdims=True)
        raised = jnp.exp(logits - peak)
        mix = raised * (1.0 / jnp.sum(raised, axis=1, keepdims=True))
        blocks[q] = jnp.where(live, mix, 0.0).astype(BF16)
        for j in range(per_seq):
            target = mixes.at[lax.div(dest[j, q], held)]
            sends.append(
                pltpu.make_async_copy(
                    blocks.at[q, pl.ds(j * block, block)], target, sems.at[q, j]
                )
            )
            sends[-1].start()

    turned[...] = stats[...].T
    lane = lax.broadcasted_iota(jnp.int32, (owned, LANES), 1)
    for k, part in enumerate(parts):
        ahead = lax.rem(line + k, side)
        mine = turned[pl.ds(pl.multiple_of(ahead * group, group), group), :]
        for n in range(side):
            target = jnp.where(core == 1, n * side + ahead, ahead * side + n)
            tag = labels[target].astype(F32)
            piece = jnp.where(lane == TAGS + line, tag, mine[n * owned : (n + 1) * owned])
            part[n, stat_rows:, :] = piece.astype(BF16)
    for send in sends:
        send.wait()


def dispatch(tokens, params, lengths, dest, place, side):
    seqs, length, width = tokens.shape[1:]
    slots = params.shape[1]
    owned = slots // (side * side)
    rows = width // LANES * seqs * owned + owned
    per_seq = dest.shape[0]
    block = length // per_seq
    return pl.pallas_call(
        dispatch_kernel,
        in_specs=[SCALARS, SCALARS, SCALARS, ANYWHERE, ANYWHERE],
        out_specs=[WHOLE] * side + [ANYWHERE],
        scratch_shapes=[
            pltpu.VMEM((width, slots), BF16),
            pltpu.VMEM((width, slots), BF16),
            pltpu.VMEM((seqs, length, width), BF16),
            pltpu.VMEM((seqs, slots, width), BF16),
            pltpu.VMEM((slots, LANES), F32),
            pltpu.VMEM((LANES, slots), F32),
            pltpu.SMEM((side * side,), jnp.int32),
            pltpu.VMEM((seqs, length, slots), BF16),
            pltpu.SemaphoreType.DMA((seqs + 1,)),
            pltpu.SemaphoreType.DMA((seqs, per_seq)),
        ],
        out_shape=[pltpu.VMEM((side, rows, LANES), BF16)] * side
        + [pltpu.HBM((side * side, block, slots), BF16)],
        compiler_params=small(24),
        name="dispatch",
    )(*in_hbm(lengths, dest), place, *in_hbm(tokens, params))


def joined_stats(raws):
    tops = [raw + pltpu.roll(raw, LANES - 1, 1) + pltpu.roll(raw, LANES - 2, 1) for raw in raws]
    top = functools.reduce(jnp.maximum, tops)
    factors = [jnp.exp(each - top) for each in tops]
    mass = sum(each * pltpu.roll(factor, 3, 1) for each, factor in zip(tops, factors))
    return top, mass, factors


def merge_kernel(place, *refs):
    side = 4
    sources, results = refs[:side], refs[side:]
    rows = sources[0].shape[1]
    owned = 16
    seqs = 4
    stat_rows = rows - owned
    slabs = stat_rows // (seqs * owned)
    lane = lax.broadcasted_iota(jnp.int32, (owned, LANES), 1)
    for k, result in enumerate(results):
        ahead = lax.rem(place[3] + k, side)
        raws = [source[ahead, stat_rows:, :].astype(F32) for source in sources]
        top, mass, factors = joined_stats(raws)
        stat = jnp.where(lane >= TAGS, sum(raws), 0.0)
        for value, first in ((top, 0), (mass, 3)):
            for n, piece in enumerate(pieces_of(value)):
                spread = pltpu.roll(piece, n, 1) if n else piece
                stat = jnp.where((lane < TAGS) & (lane % PIECES == first + n), spread, stat)
        result[stat_rows:, :] = stat.astype(BF16)
        for q in range(seqs):
            columns = [factor[:, q * PIECES : q * PIECES + 1] for factor in factors]
            for j in range(slabs):
                start = (j * seqs + q) * owned
                total = sum(
                    source[ahead, start : start + owned, :].astype(F32) * column
                    for source, column in zip(sources, columns)
                )
                result[start : start + owned, :] = total.astype(BF16)


def merge(place, parts):
    side, rows, _ = parts[0].shape
    return pl.pallas_call(
        merge_kernel,
        in_specs=[SCALARS] + [WHOLE] * side,
        out_specs=[WHOLE] * side,
        out_shape=[pltpu.VMEM((rows, LANES), BF16)] * side,
        compiler_params=small(4),
        name="merge",
    )(place, *in_vmem(*parts))


def expert_order(seqs, experts, per_expert, back):
    total = seqs * experts * per_expert
    here = lax.broadcasted_iota(jnp.int32, (total, total), 1 if back else 0)
    there = lax.broadcasted_iota(jnp.int32, (total, total), 0 if back else 1)
    expert = here // (seqs * per_expert)
    seq = here // per_expert % seqs
    rank = here % per_expert
    return (there == (seq * experts + expert) * per_expert + rank).astype(BF16)


def own_kernel(seqs, experts, *refs):
    received, (result, labels) = refs[:-2], refs[-2:]
    rows, _ = received[0].shape
    owned = result.shape[0] // seqs
    stat_rows = rows - owned
    slabs = stat_rows // (seqs * owned)
    raws = [source[stat_rows:, :].astype(F32) for source in received]
    for k, raw in enumerate(raws):
        labels[k : k + 1, :] = raw[:1]
    _, mass, factors = joined_stats(raws)
    mass = pltpu.roll(mass, LANES - 3, 1)
    parts = []
    for q in range(seqs):
        totals = [jnp.zeros((owned, LANES), F32)] * slabs
        for source, factor in zip(received, factors):
            column = (factor / mass)[:, q * PIECES : q * PIECES + 1]
            for j in range(slabs):
                start = (j * seqs + q) * owned
                totals[j] += source[start : start + owned, :].astype(F32) * column
        parts.append(jnp.concatenate(totals, axis=1))
    slot_in = jnp.concatenate(parts, axis=0).astype(BF16)
    order = expert_order(seqs, experts, owned // experts, False)
    ordered = jnp.dot(order, slot_in, preferred_element_type=F32).astype(BF16)
    result[...] = ordered


def own_slots(received, seqs, experts, owned):
    rows, _ = received[0].shape
    width = (rows - owned) // (seqs * owned) * LANES
    return pl.pallas_call(
        functools.partial(own_kernel, seqs, experts),
        in_specs=[WHOLE] * len(received),
        out_specs=[WHOLE, WHOLE],
        out_shape=[
            pltpu.VMEM((seqs * owned, width), BF16),
            jax.ShapeDtypeStruct((len(received), LANES), F32),
        ],
        compiler_params=small(4),
        name="own_slots",
    )(*in_vmem(*received))


def gelu(x):
    return 0.5 * x * (1.0 + jnp.tanh(math.sqrt(2.0 / math.pi) * (x + 0.044715 * (x * x * x))))


def expert_kernel(count, *refs):
    rows = refs[:count]
    first_far, second_far, own_out, other_out, first, second, sems = refs[count:]
    experts = first.shape[0]
    each = rows[0].shape[0] // experts
    half = count // 2
    loads = []
    for e in range(experts):
        loads.append(pltpu.make_async_copy(first_far.at[e], first.at[e], sems.at[0, e]))
        loads.append(pltpu.make_async_copy(second_far.at[e], second.at[e], sems.at[1, e]))
    for load in loads:
        load.start()
    for e in range(experts):
        span = slice(e * each, (e + 1) * each)
        both = jnp.concatenate([ref[span, :] for ref in rows], axis=0)
        loads[2 * e].wait()
        hidden = gelu(jnp.dot(both, first[e], preferred_element_type=F32)).astype(BF16)
        loads[2 * e + 1].wait()
        result = jnp.dot(hidden, second[e], preferred_element_type=F32)
        for k in range(half):
            own_out[k, span, :] = result[k * each : (k + 1) * each]
            other = result[(half + k) * each : (half + k + 1) * each]
            other_out[k, span, :] = other.astype(BF16)


def expert_layers(own, other, first, second):
    shape = (len(own), *own[0].shape)
    count = len(own) + len(other)
    return pl.pallas_call(
        functools.partial(expert_kernel, count),
        in_specs=[WHOLE] * count + [ANYWHERE, ANYWHERE],
        out_specs=[WHOLE, WHOLE],
        out_shape=[pltpu.VMEM(shape, F32), pltpu.VMEM(shape, BF16)],
        scratch_shapes=[
            pltpu.VMEM(first.shape, first.dtype),
            pltpu.VMEM(second.shape, second.dtype),
            pltpu.SemaphoreType.DMA((2, first.shape[0])),
        ],
        compiler_params=small(24),
        name="experts",
    )(*in_vmem(*own, *other), *in_hbm(first, second))


def join_kernel(own, other, kept, *sent):
    kept[...] = own[0] + other[0].astype(F32)
    for k, ref in enumerate(sent):
        ref[...] = (own[k + 1] + other[k + 1].astype(F32)).astype(BF16)


def join(own, other):
    copies, rows, width = own.shape
    return pl.pallas_call(
        join_kernel,
        in_specs=[WHOLE, WHOLE],
        out_specs=[WHOLE] * copies,
        out_shape=[pltpu.VMEM((rows, width), F32)] + [pltpu.VMEM((rows, width), BF16)] * (copies - 1),
        compiler_params=small(4),
        name="join",
    )(*in_vmem(own, other))


def collect_kernel(seqs, experts, kept, *refs):
    result = refs[-1]
    total = kept[...]
    for ref in refs[:-1]:
        total += ref[...].astype(F32)
    total = total.astype(BF16)
    per_expert = total.shape[0] // (seqs * experts)
    order = expert_order(seqs, experts, per_expert, True)
    result[...] = jnp.dot(order, total, preferred_element_type=F32).astype(BF16)


def collect(kept, parts, seqs, experts):
    return pl.pallas_call(
        functools.partial(collect_kernel, seqs, experts),
        in_specs=[WHOLE] * (1 + len(parts)),
        out_specs=WHOLE,
        out_shape=pltpu.VMEM(kept.shape, BF16),
        compiler_params=small(4),
        name="collect",
    )(*in_vmem(kept, *parts))


def stack_kernel(place, *refs):
    result = refs[-1]
    side = result.shape[0]
    for k, ref in enumerate(refs[:-1]):
        result[lax.rem(place[2] + side - k, side)] = ref[...]


def stack(place, pieces):
    return pl.pallas_call(
        stack_kernel,
        in_specs=[SCALARS] + [WHOLE] * len(pieces),
        out_specs=WHOLE,
        out_shape=pltpu.VMEM((len(pieces), *pieces[0].shape), BF16),
        compiler_params=small(4),
        name="stack",
    )(place, *in_vmem(*pieces))


def combine_kernel(source, seq, place, mix, *refs):
    lines, (result, slots, buffer, sems) = refs[:-4], refs[-4:]
    side, rows, _ = lines[0].shape
    seqs = slots.shape[0]
    owned = rows // seqs
    for k, line in enumerate(lines):
        column = lax.rem(place[3] + side - k, side) * owned
        for f in range(side):
            start = pl.multiple_of(f * side * owned + column, owned)
            for q in range(seqs):
                slots[q, pl.ds(start, owned), :] = line[f, q * owned : (q + 1) * owned, :]
    copies = []
    for b in range(result.shape[1]):
        chosen = slots[seq[b]]
        buffer[b] = jnp.dot(mix[source[b]], chosen, preferred_element_type=F32).astype(BF16)
        copies.append(pltpu.make_async_copy(buffer.at[b], result.at[0, b], sems.at[b]))
        copies[-1].start()
    for copy in copies:
        copy.wait()


def combine(source, seq, place, mixes, lines, seqs):
    _, block, slots = mixes.shape
    width = lines[0].shape[2]
    blocks = source.shape[0]
    return pl.pallas_call(
        combine_kernel,
        in_specs=[SCALARS, SCALARS, SCALARS] + [WHOLE] * (1 + len(lines)),
        out_specs=ANYWHERE,
        out_shape=pltpu.HBM((1, blocks, block, width), BF16),
        scratch_shapes=[
            pltpu.VMEM((seqs, slots, width), BF16),
            pltpu.VMEM((blocks, block, width), BF16),
            pltpu.SemaphoreType.DMA((blocks,)),
        ],
        compiler_params=small(16),
        name="combine",
    )(source, seq, place, *in_vmem(mixes, *lines))


def swapped(array):
    return lax.ppermute(array, "c", [(0, 1), (1, 0)])


def exchanged(array, axis):
    return lax.all_to_all(array, axis, split_axis=0, concat_axis=0, tiled=True)


def moved(array, axis, step):
    size = lax.axis_size(axis)
    return lax.ppermute(array, axis, [(i, (i + step) % size) for i in range(size)])


def along(array, first, step):
    side = lax.axis_size("z")
    pairs = []
    for c in range(lax.axis_size("c")):
        for z in range(side):
            for x in range(side):
                in_z = first == (c == 0)
                to_z, to_x = ((z + step) % side, x) if in_z else (z, (x + step) % side)
                pairs.append(((c * side + z) * side + x, (c * side + to_z) * side + to_x))
    return lax.ppermute(array, ("c",) + EXPERT, pairs)


def local(tokens, slot_params, dest, lengths, w_in, w_out):
    seqs, _ = tokens.shape[1:3]
    held = dest.shape[1] * dest.shape[2]
    side = lax.axis_size("z")
    experts = w_in.shape[0]
    owned = slot_params.shape[1] // (side * side)
    planes = lax.axis_size("y")
    z, x, core = lax.axis_index("z"), lax.axis_index("x"), lax.axis_index("c")
    swap = core == 1
    place = jnp.stack([z * side + x, core, jnp.where(swap, x, z), jnp.where(swap, z, x)])
    table = dest[0].T

    *parts, mixes = dispatch(tokens, slot_params, lengths, table, place, side)
    steps = range(1, side)
    parts = merge(place, [parts[0]] + [along(parts[k], True, k) for k in steps])
    received = [parts[0]] + [along(parts[k], False, k) for k in steps]
    slot_in, tags = own_slots(received, seqs, experts, owned)
    mixes, slot_in = lax.optimization_barrier((mixes, slot_in))
    arrived = exchanged(mixes, EXPERT)
    own = [slot_in] + [moved(slot_in, "y", k) for k in range(1, planes)]

    other = [swapped(piece) for piece in own]
    own_out, other_out = expert_layers(own, other, w_in, w_out)
    kept, *sent = join(own_out, swapped(other_out))
    parts = [moved(piece, "y", -k - 1) for k, piece in enumerate(sent)]
    slot_out = collect(kept, parts, seqs, experts)

    found = tags[:, TAGS : TAGS + side].astype(jnp.int32) - 1
    line = jnp.arange(side, dtype=jnp.int32)[None, :]
    across = (place[3] - jnp.arange(side, dtype=jnp.int32)[:, None]) % side
    shard = jnp.where(swap, across * side + line, line * side + across).reshape(-1)
    found = found.reshape(-1)
    block = jnp.where(found >= 0, found // seqs, -1)
    match = block[None, :] == jnp.arange(held, dtype=jnp.int32)[:, None]
    source = jnp.sum(jnp.where(match, shard[None, :], 0), axis=1)
    seq = jnp.sum(jnp.where(match, found[None, :] % seqs, 0), axis=1)

    pieces = stack(place, [slot_out] + [along(slot_out, True, k) for k in steps])
    lines = [pieces] + [along(pieces, False, k) for k in steps]
    return combine(source, seq, place, arrived, lines, seqs)


def solution(mesh):
    finer = Mesh(mesh.devices.reshape(4, 2, 4, 4), DP + EXPERT)
    in_specs = (
        P(DP, None, EXPERT, None),
        P(),
        P(DP, None, EXPERT),
        P(DP, None),
        P(EXPERT, None, DP),
        P(EXPERT, DP, None),
    )
    out_specs = P(DP, EXPERT, None, None)
    return jax.shard_map(local, mesh=finer, in_specs=in_specs, out_specs=out_specs, check_vma=False)
```

profile of v0, /device:TPU:0, one launch (start us, length us, event | category | flops | bytes accessed | tf_op | source)
XLA Modules:
  0.0 111.1 jit_solution(15663215359716562207)
XLA Ops:
  0.1 8.8 %dispatch.1 = (bf16[4,528,128]{2,1,0:T(8,128)(2,1)S(1)}, bf16[4,528,128]{2,1,0:T(8,128)(2,1)S(1)}, bf16[4,528,128]{2,1,0:T(8,128)(2,1)S(1)}, bf16[4,528,128]{2,1,0:T(8,128)(2,1)S(1)}, bf16[16,256,256]{2,1,0:T(8,128)(2,1)}) custom-call(s32[1,4]{1,0:T(1,128)} %lengths.1, s32[2,4]{1,0:T(2,128)} %bitcast.7, s32[4]{0:T(128)S(1)} %pad_add_fusion.place, ...), custom_call_target="tpu_custom_call" | custom-call | tf_op jit(solution)/shard_map/dispatch/pallas_call | solution.py:149
  8.9 2.1 %collective-permute-start = (bf16[4,528,128]{2,1,0:T(8,128)(2,1)S(1)}, bf16[4,528,128]{2,1,0:T(8,128)(2,1)S(1)}, u32[]{:S(2)}, u32[]{:S(2)}) collective-permute-start(bf16[4,528,128]{2,1,0:T(8,128)(2,1)S(1)} %get-tuple-element.25), channel_id=1, source_target_pairs={{0,4},{1,5},{2,6},{3,7},{4,8},{5,9},{6,10},{7,11},{8,12},{9,13},{1... | collective-permute-start | bytes 1622024 | tf_op jit(solution)/shard_map/ppermute | solution.py:441
  11.0 3.6 %collective-permute-start.1 = (bf16[4,528,128]{2,1,0:T(8,128)(2,1)S(1)}, bf16[4,528,128]{2,1,0:T(8,128)(2,1)S(1)}, u32[]{:S(2)}, u32[]{:S(2)}) collective-permute-start(bf16[4,528,128]{2,1,0:T(8,128)(2,1)S(1)} %get-tuple-element.26), channel_id=1, source_target_pairs={{0,8},{1,9},{2,10},{3,11},{4,12},{5,13},{6,14},{7,15},{8,0},{9,1},... | collective-permute-start | bytes 1622024 | tf_op jit(solution)/shard_map/ppermute | solution.py:441
  14.6 1.0 collective-permute-start.2
  15.6 4.9 %collective-permute-done.refs_1_ = bf16[4,528,128]{2,1,0:T(8,128)(2,1)S(1)} collective-permute-done((bf16[4,528,128]{2,1,0:T(8,128)(2,1)S(1)}, bf16[4,528,128]{2,1,0:T(8,128)(2,1)S(1)}, u32[]{:S(2)}, u32[]{:S(2)}) %collective-permute-start) | collective-permute-done | bytes 540704 | tf_op jit(solution)/shard_map/ppermute | solution.py:441
  20.5 7.2 %collective-permute-done.1.refs_2_ = bf16[4,528,128]{2,1,0:T(8,128)(2,1)S(1)} collective-permute-done((bf16[4,528,128]{2,1,0:T(8,128)(2,1)S(1)}, bf16[4,528,128]{2,1,0:T(8,128)(2,1)S(1)}, u32[]{:S(2)}, u32[]{:S(2)}) %collective-permute-start.1) | collective-permute-done | bytes 540704 | tf_op jit(solution)/shard_map/ppermute | solution.py:441
  27.7 1.5 %merge.1 = (bf16[528,128]{1,0:T(8,128)(2,1)S(1)}, bf16[528,128]{1,0:T(8,128)(2,1)S(1)}, bf16[528,128]{1,0:T(8,128)(2,1)S(1)}, bf16[528,128]{1,0:T(8,128)(2,1)S(1)}) custom-call(s32[4]{0:T(128)S(1)} %pad_add_fusion.place, bf16[4,528,128]{2,1,0:T(8,128)(2,1)S(1)} %get-tuple-element.24.refs_0_, bf16[4,528,128]{2,1,0:T(8,128)(2,1)S(1)} %collective-permute-done.refs_1_, ...), custom_call_target="tpu_custom_call" | custom-call | tf_op jit(solution)/shard_map/merge/pallas_call | solution.py:212
  29.2 1.6 %collective-permute-start.3 = (bf16[528,128]{1,0:T(8,128)(2,1)S(1)}, bf16[528,128]{1,0:T(8,128)(2,1)S(1)}, u32[]{:S(2)}, u32[]{:S(2)}) collective-permute-start(bf16[528,128]{1,0:T(8,128)(2,1)S(1)} %get-tuple-element.29), channel_id=1, source_target_pairs={{0,1},{1,2},{2,3},{3,0},{4,5},{5,6},{6,7},{7,4},{8,9},{9,10},{10,1... | collective-permute-start | bytes 405512 | tf_op jit(solution)/shard_map/ppermute | solution.py:441
  30.7 2.7 %collective-permute-start.4 = (bf16[528,128]{1,0:T(8,128)(2,1)S(1)}, bf16[528,128]{1,0:T(8,128)(2,1)S(1)}, u32[]{:S(2)}, u32[]{:S(2)}) collective-permute-start(bf16[528,128]{1,0:T(8,128)(2,1)S(1)} %get-tuple-element.30), channel_id=1, source_target_pairs={{0,2},{1,3},{2,0},{3,1},{4,6},{5,7},{6,4},{7,5},{8,10},{9,11},{10,... | collective-permute-start | bytes 405512 | tf_op jit(solution)/shard_map/ppermute | solution.py:441
  33.5 1.4 %collective-permute-start.5 = (bf16[528,128]{1,0:T(8,128)(2,1)S(1)}, bf16[528,128]{1,0:T(8,128)(2,1)S(1)}, u32[]{:S(2)}, u32[]{:S(2)}) collective-permute-start(bf16[528,128]{1,0:T(8,128)(2,1)S(1)} %get-tuple-element.31), channel_id=1, source_target_pairs={{0,3},{1,0},{2,1},{3,2},{4,7},{5,4},{6,5},{7,6},{8,11},{9,8},{10,9... | collective-permute-start | bytes 405512 | tf_op jit(solution)/shard_map/ppermute | solution.py:441
  34.9 0.6 collective-permute-done.3.refs_1_
  35.5 2.4 %collective-permute-done.4.refs_2_ = bf16[528,128]{1,0:T(8,128)(2,1)S(1)} collective-permute-done((bf16[528,128]{1,0:T(8,128)(2,1)S(1)}, bf16[528,128]{1,0:T(8,128)(2,1)S(1)}, u32[]{:S(2)}, u32[]{:S(2)}) %collective-permute-start.4) | collective-permute-done | bytes 135200 | tf_op jit(solution)/shard_map/ppermute | solution.py:441
  37.9 0.6 collective-permute-done.5.refs_3_
  38.5 0.6 own_slots.1
  39.1 6.0 %all-to-all-start = ((bf16[16,256,256]{2,1,0:T(8,128)(2,1)}), bf16[16,256,256]{2,1,0:T(8,128)(2,1)S(1)}, u32[]{:S(2)}, u32[]{:S(2)}) async-start(bf16[16,256,256]{2,1,0:T(8,128)(2,1)} %get-tuple-element.35), calls=%async_computation | async-start | bytes 4194304 | tf_op jit(solution)/shard_map/all_to_all | solution.py:424
  45.0 3.1 %collective-permute-start.8 = (bf16[64,1024]{1,0:T(8,128)(2,1)S(1)}, bf16[64,1024]{1,0:T(8,128)(2,1)S(1)}, u32[]{:S(2)}, u32[]{:S(2)}) collective-permute-start(bf16[64,1024]{1,0:T(8,128)(2,1)S(1)} %get-tuple-element.36.refs_0_), channel_id=1, source_target_pairs={{0,96},{32,0},{64,32},{96,64},{1,97},{33,1},{65,33},{97,65},{2,98}... | collective-permute-start | bytes 393224 | tf_op jit(solution)/shard_map/ppermute | solution.py:429
  48.1 0.6 collective-permute-start.7
  48.8 1.0 collective-permute-start.6
  49.7 2.3 %collective-permute-done.8.refs_3_ = bf16[64,1024]{1,0:T(8,128)(2,1)S(1)} collective-permute-done((bf16[64,1024]{1,0:T(8,128)(2,1)S(1)}, bf16[64,1024]{1,0:T(8,128)(2,1)S(1)}, u32[]{:S(2)}, u32[]{:S(2)}) %collective-permute-start.8) | collective-permute-done | bytes 131104 | tf_op jit(solution)/shard_map/ppermute | solution.py:429
  52.1 2.6 %collective-permute-done.7.refs_2_ = bf16[64,1024]{1,0:T(8,128)(2,1)S(1)} collective-permute-done((bf16[64,1024]{1,0:T(8,128)(2,1)S(1)}, bf16[64,1024]{1,0:T(8,128)(2,1)S(1)}, u32[]{:S(2)}, u32[]{:S(2)}) %collective-permute-start.7) | collective-permute-done | bytes 131104 | tf_op jit(solution)/shard_map/ppermute | solution.py:429
  54.7 1.3 %collective-permute-done.6.refs_1_ = bf16[64,1024]{1,0:T(8,128)(2,1)S(1)} collective-permute-done((bf16[64,1024]{1,0:T(8,128)(2,1)S(1)}, bf16[64,1024]{1,0:T(8,128)(2,1)S(1)}, u32[]{:S(2)}, u32[]{:S(2)}) %collective-permute-start.6) | collective-permute-done | bytes 131104 | tf_op jit(solution)/shard_map/ppermute | solution.py:429
  56.0 1.3 %collective-permute-done.10.refs_5_ = bf16[64,1024]{1,0:T(8,128)(2,1)S(1)} collective-permute-done((bf16[64,1024]{1,0:T(8,128)(2,1)S(1)}, bf16[64,1024]{1,0:T(8,128)(2,1)S(1)}, u32[]{:S(2)}, u32[]{:S(2)}) %collective-permute-start.10) | collective-permute-done | bytes 131104 | tf_op jit(solution)/shard_map/ppermute | solution.py:420
  57.4 6.5 %experts.1 = (f32[4,64,1024]{2,1,0:T(8,128)S(1)}, bf16[4,64,1024]{2,1,0:T(8,128)(2,1)S(1)}) custom-call(bf16[64,1024]{1,0:T(8,128)(2,1)S(1)} %get-tuple-element.36.refs_0_, bf16[64,1024]{1,0:T(8,128)(2,1)S(1)} %collective-permute-done.6.refs_1_, bf16[64,1024]{1,0:T(8,128)(2,1)S(1)} %collective-permute-done.7.refs_2_, ...), custom_call_target="tpu_custom_call" | custom-call | tf_op jit(solution)/shard_map/experts/pallas_call | solution.py:306
  63.9 0.2 collective-permute-start.13
  64.1 1.8 %collective-permute-done.13.other = bf16[4,64,1024]{2,1,0:T(8,128)(2,1)S(1)} collective-permute-done((bf16[4,64,1024]{2,1,0:T(8,128)(2,1)S(1)}, bf16[4,64,1024]{2,1,0:T(8,128)(2,1)S(1)}, u32[]{:S(2)}, u32[]{:S(2)}) %collective-permute-start.13) | collective-permute-done | bytes 524320 | tf_op jit(solution)/shard_map/ppermute | solution.py:420
  65.9 0.1 join.1
  66.0 0.6 collective-permute-start.14
  66.6 0.6 collective-permute-start.15
  67.2 0.9 collective-permute-start.16
  68.1 4.3 %collective-permute-done.14.refs_0_ = bf16[64,1024]{1,0:T(8,128)(2,1)S(1)} collective-permute-done((bf16[64,1024]{1,0:T(8,128)(2,1)S(1)}, bf16[64,1024]{1,0:T(8,128)(2,1)S(1)}, u32[]{:S(2)}, u32[]{:S(2)}) %collective-permute-start.14) | collective-permute-done | bytes 131104 | tf_op jit(solution)/shard_map/ppermute | solution.py:429
  72.4 2.0 %collective-permute-done.15.refs_1_ = bf16[64,1024]{1,0:T(8,128)(2,1)S(1)} collective-permute-done((bf16[64,1024]{1,0:T(8,128)(2,1)S(1)}, bf16[64,1024]{1,0:T(8,128)(2,1)S(1)}, u32[]{:S(2)}, u32[]{:S(2)}) %collective-permute-start.15) | collective-permute-done | bytes 131104 | tf_op jit(solution)/shard_map/ppermute | solution.py:429
  74.4 1.8 %collective-permute-done.16.refs_2_ = bf16[64,1024]{1,0:T(8,128)(2,1)S(1)} collective-permute-done((bf16[64,1024]{1,0:T(8,128)(2,1)S(1)}, bf16[64,1024]{1,0:T(8,128)(2,1)S(1)}, u32[]{:S(2)}, u32[]{:S(2)}) %collective-permute-start.16) | collective-permute-done | bytes 131104 | tf_op jit(solution)/shard_map/ppermute | solution.py:429
  76.2 0.2 collect.1.refs_0_
  76.4 3.1 %collective-permute-start.19 = (bf16[64,1024]{1,0:T(8,128)(2,1)S(1)}, bf16[64,1024]{1,0:T(8,128)(2,1)S(1)}, u32[]{:S(2)}, u32[]{:S(2)}) collective-permute-start(bf16[64,1024]{1,0:T(8,128)(2,1)S(1)} %collect.1.refs_0_), channel_id=1, source_target_pairs={{0,12},{1,13},{2,14},{3,15},{4,0},{5,1},{6,2},{7,3},{8,4},{9,5},{1... | collective-permute-start | bytes 393224 | tf_op jit(solution)/shard_map/ppermute | solution.py:441
  79.5 0.9 collective-permute-start.18
  80.4 0.9 collective-permute-start.17
  81.3 0.1 select_n.78
  81.4 0.7 collective-permute-done.19.refs_3_
  82.1 4.0 %collective-permute-done.18.refs_2_ = bf16[64,1024]{1,0:T(8,128)(2,1)S(1)} collective-permute-done((bf16[64,1024]{1,0:T(8,128)(2,1)S(1)}, bf16[64,1024]{1,0:T(8,128)(2,1)S(1)}, u32[]{:S(2)}, u32[]{:S(2)}) %collective-permute-start.18) | collective-permute-done | bytes 131104 | tf_op jit(solution)/shard_map/ppermute | solution.py:441
  86.1 1.3 %collective-permute-done.17.refs_1_ = bf16[64,1024]{1,0:T(8,128)(2,1)S(1)} collective-permute-done((bf16[64,1024]{1,0:T(8,128)(2,1)S(1)}, bf16[64,1024]{1,0:T(8,128)(2,1)S(1)}, u32[]{:S(2)}, u32[]{:S(2)}) %collective-permute-start.17) | collective-permute-done | bytes 131104 | tf_op jit(solution)/shard_map/ppermute | solution.py:441
  87.4 0.6 stack.21.refs_0_
  88.0 2.7 %collective-permute-start.22 = (bf16[4,64,1024]{2,1,0:T(8,128)(2,1)S(1)}, bf16[4,64,1024]{2,1,0:T(8,128)(2,1)S(1)}, u32[]{:S(2)}, u32[]{:S(2)}) collective-permute-start(bf16[4,64,1024]{2,1,0:T(8,128)(2,1)S(1)} %stack.21.refs_0_), channel_id=1, source_target_pairs={{0,3},{1,0},{2,1},{3,2},{4,7},{5,4},{6,5},{7,6},{8,11},{9,8},{10,9... | collective-permute-start | bytes 1572872 | tf_op jit(solution)/shard_map/ppermute | solution.py:441
  90.8 0.9 collective-permute-start.21
  91.6 0.9 collective-permute-start.20
  92.6 0.1 select_reduce_fusion
  92.8 10.3 %collective-permute-done.22.refs_3_ = bf16[4,64,1024]{2,1,0:T(8,128)(2,1)S(1)} collective-permute-done((bf16[4,64,1024]{2,1,0:T(8,128)(2,1)S(1)}, bf16[4,64,1024]{2,1,0:T(8,128)(2,1)S(1)}, u32[]{:S(2)}, u32[]{:S(2)}) %collective-permute-start.22) | collective-permute-done | bytes 524320 | tf_op jit(solution)/shard_map/ppermute | solution.py:441
  103.1 4.1 %collective-permute-done.20.refs_1_ = bf16[4,64,1024]{2,1,0:T(8,128)(2,1)} collective-permute-done((bf16[4,64,1024]{2,1,0:T(8,128)(2,1)S(1)}, bf16[4,64,1024]{2,1,0:T(8,128)(2,1)}, u32[]{:S(2)}, u32[]{:S(2)}) %collective-permute-start.20) | collective-permute-done | bytes 524320 | tf_op jit(solution)/shard_map/ppermute | solution.py:441
  107.2 3.7 %combine.1 = bf16[1,8,256,1024]{3,2,1,0:T(8,128)(2,1)} custom-call(s32[8]{0:T(128)S(1)} %get-tuple-element.44.source, s32[8]{0:T(128)S(1)} %get-tuple-element.43.seq, s32[4]{0:T(128)S(1)} %pad_add_fusion.place, bf16[16,256,256]{2,1,0:T(8,128)(2,1)S(1)} %all-to-all-done.mix, bf16[4,64,1024]{2,1,0:T(8,128)(2,1)S(1)} %stack.21.refs_0_, ...), custom_call_target="tpu_custom_call" | custom-call | tf_op jit(solution)/shard_map/combine/pallas_call | solution.py:404
  (17 shorter events, 0.4 us)
Async XLA Ops:
  8.9 11.6 %collective-permute-start = (bf16[4,528,128]{2,1,0:T(8,128)(2,1)S(1)}, bf16[4,528,128]{2,1,0:T(8,128)(2,1)S(1)}, u32[]{:S(2)}, u32[]{:S(2)}) collective-permute-start(bf16[4,528,128]{2,1,0:T(8,128)(2,1)S(1)} %get-tuple-element.25), channel_id=1, source_target_pairs={{0,4},{1,5},{2,6},{3,7},{4,8},{5,9},{6,10},{7,11},{8,12},{9,13},{1... | collective-permute-start | bytes 1622024 | tf_op jit(solution)/shard_map/ppermute | solution.py:441
  11.0 16.7 %collective-permute-start.1 = (bf16[4,528,128]{2,1,0:T(8,128)(2,1)S(1)}, bf16[4,528,128]{2,1,0:T(8,128)(2,1)S(1)}, u32[]{:S(2)}, u32[]{:S(2)}) collective-permute-start(bf16[4,528,128]{2,1,0:T(8,128)(2,1)S(1)} %get-tuple-element.26), channel_id=1, source_target_pairs={{0,8},{1,9},{2,10},{3,11},{4,12},{5,13},{6,14},{7,15},{8,0},{9,1},... | collective-permute-start | bytes 1622024 | tf_op jit(solution)/shard_map/ppermute | solution.py:441
  14.6 13.1 %collective-permute-start.2 = (bf16[4,528,128]{2,1,0:T(8,128)(2,1)S(1)}, bf16[4,528,128]{2,1,0:T(8,128)(2,1)S(1)}, u32[]{:S(2)}, u32[]{:S(2)}) collective-permute-start(bf16[4,528,128]{2,1,0:T(8,128)(2,1)S(1)} %get-tuple-element.27), channel_id=1, source_target_pairs={{0,12},{1,13},{2,14},{3,15},{4,0},{5,1},{6,2},{7,3},{8,4},{9,5},{1... | collective-permute-start | bytes 1622024 | tf_op jit(solution)/shard_map/ppermute | solution.py:441
  29.2 6.3 %collective-permute-start.3 = (bf16[528,128]{1,0:T(8,128)(2,1)S(1)}, bf16[528,128]{1,0:T(8,128)(2,1)S(1)}, u32[]{:S(2)}, u32[]{:S(2)}) collective-permute-start(bf16[528,128]{1,0:T(8,128)(2,1)S(1)} %get-tuple-element.29), channel_id=1, source_target_pairs={{0,1},{1,2},{2,3},{3,0},{4,5},{5,6},{6,7},{7,4},{8,9},{9,10},{10,1... | collective-permute-start | bytes 405512 | tf_op jit(solution)/shard_map/ppermute | solution.py:441
  30.7 7.2 %collective-permute-start.4 = (bf16[528,128]{1,0:T(8,128)(2,1)S(1)}, bf16[528,128]{1,0:T(8,128)(2,1)S(1)}, u32[]{:S(2)}, u32[]{:S(2)}) collective-permute-start(bf16[528,128]{1,0:T(8,128)(2,1)S(1)} %get-tuple-element.30), channel_id=1, source_target_pairs={{0,2},{1,3},{2,0},{3,1},{4,6},{5,7},{6,4},{7,5},{8,10},{9,11},{10,... | collective-permute-start | bytes 405512 | tf_op jit(solution)/shard_map/ppermute | solution.py:441
  33.5 5.0 %collective-permute-start.5 = (bf16[528,128]{1,0:T(8,128)(2,1)S(1)}, bf16[528,128]{1,0:T(8,128)(2,1)S(1)}, u32[]{:S(2)}, u32[]{:S(2)}) collective-permute-start(bf16[528,128]{1,0:T(8,128)(2,1)S(1)} %get-tuple-element.31), channel_id=1, source_target_pairs={{0,3},{1,0},{2,1},{3,2},{4,7},{5,4},{6,5},{7,6},{8,11},{9,8},{10,9... | collective-permute-start | bytes 405512 | tf_op jit(solution)/shard_map/ppermute | solution.py:441
  39.1 68.1 %all-to-all-start = ((bf16[16,256,256]{2,1,0:T(8,128)(2,1)}), bf16[16,256,256]{2,1,0:T(8,128)(2,1)S(1)}, u32[]{:S(2)}, u32[]{:S(2)}) async-start(bf16[16,256,256]{2,1,0:T(8,128)(2,1)} %get-tuple-element.35), calls=%async_computation | async-start | bytes 4194304 | tf_op jit(solution)/shard_map/all_to_all | solution.py:424
  45.0 7.0 %collective-permute-start.8 = (bf16[64,1024]{1,0:T(8,128)(2,1)S(1)}, bf16[64,1024]{1,0:T(8,128)(2,1)S(1)}, u32[]{:S(2)}, u32[]{:S(2)}) collective-permute-start(bf16[64,1024]{1,0:T(8,128)(2,1)S(1)} %get-tuple-element.36.refs_0_), channel_id=1, source_target_pairs={{0,96},{32,0},{64,32},{96,64},{1,97},{33,1},{65,33},{97,65},{2,98}... | collective-permute-start | bytes 393224 | tf_op jit(solution)/shard_map/ppermute | solution.py:429
  48.1 6.6 %collective-permute-start.7 = (bf16[64,1024]{1,0:T(8,128)(2,1)S(1)}, bf16[64,1024]{1,0:T(8,128)(2,1)S(1)}, u32[]{:S(2)}, u32[]{:S(2)}) collective-permute-start(bf16[64,1024]{1,0:T(8,128)(2,1)S(1)} %get-tuple-element.36.refs_0_), channel_id=1, source_target_pairs={{0,64},{32,96},{64,0},{96,32},{1,65},{33,97},{65,1},{97,33},{2,66}... | collective-permute-start | bytes 393224 | tf_op jit(solution)/shard_map/ppermute | solution.py:429
  48.8 7.2 %collective-permute-start.6 = (bf16[64,1024]{1,0:T(8,128)(2,1)S(1)}, bf16[64,1024]{1,0:T(8,128)(2,1)S(1)}, u32[]{:S(2)}, u32[]{:S(2)}) collective-permute-start(bf16[64,1024]{1,0:T(8,128)(2,1)S(1)} %get-tuple-element.36.refs_0_), channel_id=1, source_target_pairs={{0,32},{32,64},{64,96},{96,0},{1,33},{33,65},{65,97},{97,1},{2,34}... | collective-permute-start | bytes 393224 | tf_op jit(solution)/shard_map/ppermute | solution.py:429
  49.7 6.3 %collective-permute-start.9 = (bf16[64,1024]{1,0:T(8,128)(2,1)S(1)}, bf16[64,1024]{1,0:T(8,128)(2,1)S(1)}, u32[]{:S(2)}, u32[]{:S(2)}) collective-permute-start(bf16[64,1024]{1,0:T(8,128)(2,1)S(1)} %get-tuple-element.36.refs_0_), channel_id=1, source_target_pairs={{0,16},{16,0},{1,17},{17,1},{2,18},{18,2},{3,19},{19,3},{4,20},{20... | collective-permute-start | bytes 393224 | tf_op jit(solution)/shard_map/ppermute | solution.py:420
  52.1 4.0 %collective-permute-start.12 = (bf16[64,1024]{1,0:T(8,128)(2,1)S(1)}, bf16[64,1024]{1,0:T(8,128)(2,1)S(1)}, u32[]{:S(2)}, u32[]{:S(2)}) collective-permute-start(bf16[64,1024]{1,0:T(8,128)(2,1)S(1)} %collective-permute-done.8.refs_3_), channel_id=1, source_target_pairs={{0,16},{16,0},{1,17},{17,1},{2,18},{18,2},{3,19},{19,3},{4,20},{20... | collective-permute-start | bytes 393224 | tf_op jit(solution)/shard_map/ppermute | solution.py:420
  54.7 1.3 %collective-permute-start.11 = (bf16[64,1024]{1,0:T(8,128)(2,1)S(1)}, bf16[64,1024]{1,0:T(8,128)(2,1)S(1)}, u32[]{:S(2)}, u32[]{:S(2)}) collective-permute-start(bf16[64,1024]{1,0:T(8,128)(2,1)S(1)} %collective-permute-done.7.refs_2_), channel_id=1, source_target_pairs={{0,16},{16,0},{1,17},{17,1},{2,18},{18,2},{3,19},{19,3},{4,20},{20... | collective-permute-start | bytes 393224 | tf_op jit(solution)/shard_map/ppermute | solution.py:420
  56.0 1.3 %collective-permute-start.10 = (bf16[64,1024]{1,0:T(8,128)(2,1)S(1)}, bf16[64,1024]{1,0:T(8,128)(2,1)S(1)}, u32[]{:S(2)}, u32[]{:S(2)}) collective-permute-start(bf16[64,1024]{1,0:T(8,128)(2,1)S(1)} %collective-permute-done.6.refs_1_), channel_id=1, source_target_pairs={{0,16},{16,0},{1,17},{17,1},{2,18},{18,2},{3,19},{19,3},{4,20},{20... | collective-permute-start | bytes 393224 | tf_op jit(solution)/shard_map/ppermute | solution.py:420
  63.9 2.0 %collective-permute-start.13 = (bf16[4,64,1024]{2,1,0:T(8,128)(2,1)S(1)}, bf16[4,64,1024]{2,1,0:T(8,128)(2,1)S(1)}, u32[]{:S(2)}, u32[]{:S(2)}) collective-permute-start(bf16[4,64,1024]{2,1,0:T(8,128)(2,1)S(1)} %get-tuple-element.38), channel_id=1, source_target_pairs={{0,16},{16,0},{1,17},{17,1},{2,18},{18,2},{3,19},{19,3},{4,20},{20... | collective-permute-start | bytes 1572872 | tf_op jit(solution)/shard_map/ppermute | solution.py:420
  66.0 6.4 %collective-permute-start.14 = (bf16[64,1024]{1,0:T(8,128)(2,1)S(1)}, bf16[64,1024]{1,0:T(8,128)(2,1)S(1)}, u32[]{:S(2)}, u32[]{:S(2)}) collective-permute-start(bf16[64,1024]{1,0:T(8,128)(2,1)S(1)} %get-tuple-element.40), channel_id=1, source_target_pairs={{0,96},{32,0},{64,32},{96,64},{1,97},{33,1},{65,33},{97,65},{2,98}... | collective-permute-start | bytes 393224 | tf_op jit(solution)/shard_map/ppermute | solution.py:429
  66.6 7.8 %collective-permute-start.15 = (bf16[64,1024]{1,0:T(8,128)(2,1)S(1)}, bf16[64,1024]{1,0:T(8,128)(2,1)S(1)}, u32[]{:S(2)}, u32[]{:S(2)}) collective-permute-start(bf16[64,1024]{1,0:T(8,128)(2,1)S(1)} %get-tuple-element.41), channel_id=1, source_target_pairs={{0,64},{32,96},{64,0},{96,32},{1,65},{33,97},{65,1},{97,33},{2,66}... | collective-permute-start | bytes 393224 | tf_op jit(solution)/shard_map/ppermute | solution.py:429
  67.2 9.0 %collective-permute-start.16 = (bf16[64,1024]{1,0:T(8,128)(2,1)S(1)}, bf16[64,1024]{1,0:T(8,128)(2,1)S(1)}, u32[]{:S(2)}, u32[]{:S(2)}) collective-permute-start(bf16[64,1024]{1,0:T(8,128)(2,1)S(1)} %get-tuple-element.42), channel_id=1, source_target_pairs={{0,32},{32,64},{64,96},{96,0},{1,33},{33,65},{65,97},{97,1},{2,34}... | collective-permute-start | bytes 393224 | tf_op jit(solution)/shard_map/ppermute | solution.py:429
  76.4 5.7 %collective-permute-start.19 = (bf16[64,1024]{1,0:T(8,128)(2,1)S(1)}, bf16[64,1024]{1,0:T(8,128)(2,1)S(1)}, u32[]{:S(2)}, u32[]{:S(2)}) collective-permute-start(bf16[64,1024]{1,0:T(8,128)(2,1)S(1)} %collect.1.refs_0_), channel_id=1, source_target_pairs={{0,12},{1,13},{2,14},{3,15},{4,0},{5,1},{6,2},{7,3},{8,4},{9,5},{1... | collective-permute-start | bytes 393224 | tf_op jit(solution)/shard_map/ppermute | solution.py:441
  79.5 6.6 %collective-permute-start.18 = (bf16[64,1024]{1,0:T(8,128)(2,1)S(1)}, bf16[64,1024]{1,0:T(8,128)(2,1)S(1)}, u32[]{:S(2)}, u32[]{:S(2)}) collective-permute-start(bf16[64,1024]{1,0:T(8,128)(2,1)S(1)} %collect.1.refs_0_), channel_id=1, source_target_pairs={{0,8},{1,9},{2,10},{3,11},{4,12},{5,13},{6,14},{7,15},{8,0},{9,1},... | collective-permute-start | bytes 393224 | tf_op jit(solution)/shard_map/ppermute | solution.py:441
  80.4 7.0 %collective-permute-start.17 = (bf16[64,1024]{1,0:T(8,128)(2,1)S(1)}, bf16[64,1024]{1,0:T(8,128)(2,1)S(1)}, u32[]{:S(2)}, u32[]{:S(2)}) collective-permute-start(bf16[64,1024]{1,0:T(8,128)(2,1)S(1)} %collect.1.refs_0_), channel_id=1, source_target_pairs={{0,4},{1,5},{2,6},{3,7},{4,8},{5,9},{6,10},{7,11},{8,12},{9,13},{1... | collective-permute-start | bytes 393224 | tf_op jit(solution)/shard_map/ppermute | solution.py:441
  88.0 15.1 %collective-permute-start.22 = (bf16[4,64,1024]{2,1,0:T(8,128)(2,1)S(1)}, bf16[4,64,1024]{2,1,0:T(8,128)(2,1)S(1)}, u32[]{:S(2)}, u32[]{:S(2)}) collective-permute-start(bf16[4,64,1024]{2,1,0:T(8,128)(2,1)S(1)} %stack.21.refs_0_), channel_id=1, source_target_pairs={{0,3},{1,0},{2,1},{3,2},{4,7},{5,4},{6,5},{7,6},{8,11},{9,8},{10,9... | collective-permute-start | bytes 1572872 | tf_op jit(solution)/shard_map/ppermute | solution.py:441
  90.8 12.4 %collective-permute-start.21 = (bf16[4,64,1024]{2,1,0:T(8,128)(2,1)S(1)}, bf16[4,64,1024]{2,1,0:T(8,128)(2,1)}, u32[]{:S(2)}, u32[]{:S(2)}) collective-permute-start(bf16[4,64,1024]{2,1,0:T(8,128)(2,1)S(1)} %stack.21.refs_0_), channel_id=1, source_target_pairs={{0,2},{1,3},{2,0},{3,1},{4,6},{5,7},{6,4},{7,5},{8,10},{9,11},{10,... | collective-permute-start | bytes 1572872 | tf_op jit(solution)/shard_map/ppermute | solution.py:441
  91.6 15.6 %collective-permute-start.20 = (bf16[4,64,1024]{2,1,0:T(8,128)(2,1)S(1)}, bf16[4,64,1024]{2,1,0:T(8,128)(2,1)}, u32[]{:S(2)}, u32[]{:S(2)}) collective-permute-start(bf16[4,64,1024]{2,1,0:T(8,128)(2,1)S(1)} %stack.21.refs_0_), channel_id=1, source_target_pairs={{0,1},{1,2},{2,3},{3,0},{4,5},{5,6},{6,7},{7,4},{8,9},{9,10},{10,1... | collective-permute-start | bytes 1572872 | tf_op jit(solution)/shard_map/ppermute | solution.py:441
where the time goes:
time: 111 us
  waiting for transfers between devices  53.5 us (48%)
  starting transfers between devices  34.7 us (31%)
  Pallas kernels  22 us (20%)
    ppermute x12, waiting for transfers between devices, along(): return lax.ppermute(array, ('c',) + EXPERT, pairs)  36.1 us
    ppermute x12, starting transfers between devices, along(): return lax.ppermute(array, ('c',) + EXPERT, pairs)  21.7 us
    ppermute x6, waiting for transfers between devices, moved(): lax.ppermute(array, axis, [(i, (i + step) % size) for i in range(size)])  14.3 us
    pallas_call x1, Pallas kernels, dispatch(): pl.pallas_call(dispatch_kernel, in_specs=[SCALARS, SCALARS, SCALARS, ANYW...  8.83 us
    ppermute x6, starting transfers between devices, moved(): lax.ppermute(array, axis, [(i, (i + step) % size) for i in range(size)])  6.81 us
    pallas_call x1, Pallas kernels, expert_layers(): pl.pallas_call(functools.partial(expert_kernel, count), in_specs=[WHOLE]...  6.53 us
    all_to_all x1, starting transfers between devices, exchanged(): return lax.all_to_all(array, axis, split_axis=0, concat_axis=0, tiled=True)  5.97 us
    pallas_call x1, Pallas kernels, combine(): pl.pallas_call(combine_kernel, in_specs=[SCALARS, SCALARS, SCALARS] + [WH...  3.73 us
  transfers between devices with their start and end apart: 24, of which 18 were waited for; matrix products, arithmetic and copies ran while one was open for 0% of the time, Pallas kernels for 7%

commit v1 on v0

--- a/solution.py
+++ b/solution.py
@@ -56,15 +56,14 @@
 def dispatch_kernel(lengths, dest, place, tokens, params, *refs):
     side = 4
     parts = refs[:side]
-    mixes, plain, order, held_tokens, sums, turned, stats, labels, blocks, loads, sems = refs[side:]
+    plain, order, held_tokens, sums, turned, stats, labels, loads = refs[side:]
     shard, core, line = place[0], place[1], place[2]
     _, seqs, length, width = tokens.shape
     slots = params.shape[1]
     owned = slots // (side * side)
     slabs = width // LANES
     stat_rows = parts[0].shape[1] - owned
-    block = mixes.shape[1]
-    per_seq = length // block
+    per_seq = dest.shape[0]
     held = per_seq * seqs
     group = side * owned
 
@@ -85,7 +84,6 @@
     first_load.wait()
     order[...] = jnp.dot(plain[...], sorting, preferred_element_type=F32).astype(BF16)
 
-    sends = []
     row = lax.broadcasted_iota(jnp.int32, (PIECES, slots), 0)
     for q in range(seqs):
         arrivals[q].wait()
@@ -112,6 +110,40 @@
             stacked = jnp.where(row == k, piece, stacked)
         stats[q * PIECES : (q + 1) * PIECES, :] = stacked
 
+    turned[...] = stats[...].T
+    lane = lax.broadcasted_iota(jnp.int32, (owned, LANES), 1)
+    for k, part in enumerate(parts):
+        ahead = lax.rem(line + k, side)
+        mine = turned[pl.ds(pl.multiple_of(ahead * group, group), group), :]
+        for n in range(side):
+            target = jnp.where(core == 1, n * side + ahead, ahead * side + n)
+            tag = labels[target].astype(F32)
+            piece = jnp.where(lane == TAGS + line, tag, mine[n * owned : (n + 1) * owned])
+            part[n, stat_rows:, :] = piece.astype(BF16)
+
+
+def mix_kernel(lengths, dest, place, tokens, params, mixes, plain, held_tokens, blocks, loads, sems):
+    shard, core = place[0], place[1]
+    _, seqs, length, _ = tokens.shape
+    slots = params.shape[1]
+    block = mixes.shape[1]
+    per_seq = length // block
+    held = per_seq * seqs
+    first_load = pltpu.make_async_copy(params, plain, loads.at[seqs])
+    first_load.start()
+    arrivals = []
+    for q in range(seqs):
+        arrivals.append(pltpu.make_async_copy(tokens.at[0, q], held_tokens.at[q], loads.at[q]))
+        arrivals[-1].start()
+    sorting = line_order(slots, slots // mixes.shape[0], core == 1)
+    first_load.wait()
+    order = jnp.dot(plain[...], sorting, preferred_element_type=F32).astype(BF16)
+    sends = []
+    for q in range(seqs):
+        arrivals[q].wait()
+        logits = jnp.dot(held_tokens[q], order, preferred_element_type=F32)
+        count = lengths[0, q] - shard * length
+        live = lax.broadcasted_iota(jnp.int32, (length, 1), 0) < count
         peak = jnp.max(logits, axis=1, keepdims=True)
         raised = jnp.exp(logits - peak)
         mix = raised * (1.0 / jnp.sum(raised, axis=1, keepdims=True))
@@ -124,19 +156,29 @@
                 )
             )
             sends[-1].start()
-
-    turned[...] = stats[...].T
-    lane = lax.broadcasted_iota(jnp.int32, (owned, LANES), 1)
-    for k, part in enumerate(parts):
-        ahead = lax.rem(line + k, side)
-        mine = turned[pl.ds(pl.multiple_of(ahead * group, group), group), :]
-        for n in range(side):
-            target = jnp.where(core == 1, n * side + ahead, ahead * side + n)
-            tag = labels[target].astype(F32)
-            piece = jnp.where(lane == TAGS + line, tag, mine[n * owned : (n + 1) * owned])
-            part[n, stat_rows:, :] = piece.astype(BF16)
     for send in sends:
         send.wait()
+
+
+def mix_rows(tokens, params, lengths, dest, place, side):
+    _, seqs, length, width = tokens.shape
+    slots = params.shape[1]
+    per_seq = dest.shape[0]
+    return pl.pallas_call(
+        mix_kernel,
+        in_specs=[SCALARS, SCALARS, SCALARS, ANYWHERE, ANYWHERE],
+        out_specs=ANYWHERE,
+        scratch_shapes=[
+            pltpu.VMEM((width, slots), BF16),
+            pltpu.VMEM((seqs, length, width), BF16),
+            pltpu.VMEM((seqs, length, slots), BF16),
+            pltpu.SemaphoreType.DMA((seqs + 1,)),
+            pltpu.SemaphoreType.DMA((seqs, per_seq)),
+        ],
+        out_shape=pltpu.HBM((side * side, length // per_seq, slots), BF16),
+        compiler_params=small(16),
+        name="mix_rows",
+    )(*in_hbm(lengths, dest), place, *in_hbm(tokens, params))
 
 
 def dispatch(tokens, params, lengths, dest, place, side):
@@ -144,12 +186,10 @@
     slots = params.shape[1]
     owned = slots // (side * side)
     rows = width // LANES * seqs * owned + owned
-    per_seq = dest.shape[0]
-    block = length // per_seq
     return pl.pallas_call(
         dispatch_kernel,
         in_specs=[SCALARS, SCALARS, SCALARS, ANYWHERE, ANYWHERE],
-        out_specs=[WHOLE] * side + [ANYWHERE],
+        out_specs=[WHOLE] * side,
         scratch_shapes=[
             pltpu.VMEM((width, slots), BF16),
             pltpu.VMEM((width, slots), BF16),
@@ -158,12 +198,9 @@
             pltpu.VMEM((slots, LANES), F32),
             pltpu.VMEM((LANES, slots), F32),
             pltpu.SMEM((side * side,), jnp.int32),
-            pltpu.VMEM((seqs, length, slots), BF16),
             pltpu.SemaphoreType.DMA((seqs + 1,)),
-            pltpu.SemaphoreType.DMA((seqs, per_seq)),
         ],
-        out_shape=[pltpu.VMEM((side, rows, LANES), BF16)] * side
-        + [pltpu.HBM((side * side, block, slots), BF16)],
+        out_shape=[pltpu.VMEM((side, rows, LANES), BF16)] * side,
         compiler_params=small(24),
         name="dispatch",
     )(*in_hbm(lengths, dest), place, *in_hbm(tokens, params))
@@ -275,24 +312,39 @@
     return 0.5 * x * (1.0 + jnp.tanh(math.sqrt(2.0 / math.pi) * (x + 0.044715 * (x * x * x))))
 
 
+def fetch_kernel(first, second, first_out, second_out, sems):
+    copies = []
+    for e in range(first.shape[0]):
+        copies.append(pltpu.make_async_copy(first.at[e], first_out.at[e], sems.at[0, e]))
+        copies.append(pltpu.make_async_copy(second.at[e], second_out.at[e], sems.at[1, e]))
+    for copy in copies:
+        copy.start()
+    for copy in copies:
+        copy.wait()
+
+
+def fetch(first, second):
+    return pl.pallas_call(
+        fetch_kernel,
+        in_specs=[ANYWHERE, ANYWHERE],
+        out_specs=[WHOLE, WHOLE],
+        out_shape=[pltpu.VMEM(first.shape, first.dtype), pltpu.VMEM(second.shape, second.dtype)],
+        scratch_shapes=[pltpu.SemaphoreType.DMA((2, first.shape[0]))],
+        compiler_params=small(1),
+        name="fetch",
+    )(*in_hbm(first, second))
+
+
 def expert_kernel(count, *refs):
     rows = refs[:count]
-    first_far, second_far, own_out, other_out, first, second, sems = refs[count:]
+    first, second, own_out, other_out = refs[count:]
     experts = first.shape[0]
     each = rows[0].shape[0] // experts
     half = count // 2
-    loads = []
-    for e in range(experts):
-        loads.append(pltpu.make_async_copy(first_far.at[e], first.at[e], sems.at[0, e]))
-        loads.append(pltpu.make_async_copy(second_far.at[e], second.at[e], sems.at[1, e]))
-    for load in loads:
-        load.start()
     for e in range(experts):
         span = slice(e * each, (e + 1) * each)
         both = jnp.concatenate([ref[span, :] for ref in rows], axis=0)
-        loads[2 * e].wait()
         hidden = gelu(jnp.dot(both, first[e], preferred_element_type=F32)).astype(BF16)
-        loads[2 * e + 1].wait()
         result = jnp.dot(hidden, second[e], preferred_element_type=F32)
         for k in range(half):
             own_out[k, span, :] = result[k * each : (k + 1) * each]
@@ -305,17 +357,12 @@
     count = len(own) + len(other)
     return pl.pallas_call(
         functools.partial(expert_kernel, count),
-        in_specs=[WHOLE] * count + [ANYWHERE, ANYWHERE],
+        in_specs=[WHOLE] * (count + 2),
         out_specs=[WHOLE, WHOLE],
         out_shape=[pltpu.VMEM(shape, F32), pltpu.VMEM(shape, BF16)],
-        scratch_shapes=[
-            pltpu.VMEM(first.shape, first.dtype),
-            pltpu.VMEM(second.shape, second.dtype),
-            pltpu.SemaphoreType.DMA((2, first.shape[0])),
-        ],
-        compiler_params=small(24),
+        compiler_params=small(8),
         name="experts",
-    )(*in_vmem(*own, *other), *in_hbm(first, second))
+    )(*in_vmem(*own, *other, first, second))
 
 
 def join_kernel(own, other, kept, *sent):
@@ -453,17 +500,20 @@
     place = jnp.stack([z * side + x, core, jnp.where(swap, x, z), jnp.where(swap, z, x)])
     table = dest[0].T
 
-    *parts, mixes = dispatch(tokens, slot_params, lengths, table, place, side)
     steps = range(1, side)
-    parts = merge(place, [parts[0]] + [along(parts[k], True, k) for k in steps])
+    parts = dispatch(tokens, slot_params, lengths, table, place, side)
+    mixes = mix_rows(tokens, slot_params, lengths, table, place, side)
+    parts = [parts[0]] + [along(parts[k], True, k) for k in steps]
+    parts = merge(place, parts)
+    mixes, *parts = lax.optimization_barrier((mixes, *parts))
     received = [parts[0]] + [along(parts[k], False, k) for k in steps]
+    arrived = exchanged(mixes, EXPERT)
     slot_in, tags = own_slots(received, seqs, experts, owned)
-    mixes, slot_in = lax.optimization_barrier((mixes, slot_in))
-    arrived = exchanged(mixes, EXPERT)
+    weights = fetch(w_in, w_out)
     own = [slot_in] + [moved(slot_in, "y", k) for k in range(1, planes)]
 
     other = [swapped(piece) for piece in own]
-    own_out, other_out = expert_layers(own, other, w_in, w_out)
+    own_out, other_out = expert_layers(own, other, *weights)
     kept, *sent = join(own_out, swapped(other_out))
     parts = [moved(piece, "y", -k - 1) for k, piece in enumerate(sent)]
     slot_out = collect(kept, parts, seqs, experts)

time: 111 us -> 132 us (1.19)
  waiting for transfers between devices: 53.5 us -> 66.6 us
  Pallas kernels: 22 us -> 30.9 us
  starting transfers between devices: 34.7 us -> 33 us
    ppermute x12, waiting for transfers between devices: 36.1 us -> 50.5 us  [along(): return lax.ppermute(array, ('c',) + EXPERT, pairs)]
    pallas_call x0 -> x2, Pallas kernels: none -> 12.3 us  [the longest x1 6.33 us: mix_rows(): pl.pallas_call(mix_kernel, in_specs=[SCALARS, SCALARS, SCALARS, ANYWHERE,...]
    pallas_call x1, Pallas kernels: 6.53 us -> 3.82 us  [expert_layers(): pl.pallas_call(functools.partial(expert_kernel, count), in_specs=[WHOLE]...]
    ppermute x12, starting transfers between devices: 21.7 us -> 19.2 us  [along(): return lax.ppermute(array, ('c',) + EXPERT, pairs)]
    ppermute x5, waiting for transfers between devices: 3.1 us -> 1.55 us  [swapped(): return lax.ppermute(array, 'c', [(0, 1), (1, 0)])]
  transfers between devices with their start and end apart: 24 -> 24, of which waited for: 18 -> 16; matrix products, arithmetic and copies ran while one was open for 0% -> 0% of each run, Pallas kernels for 7% -> 13%
where the time goes in v1:
time: 132 us; the launch traced here: 131 us
  waiting for transfers between devices  66.6 us (50%)
  starting transfers between devices  33 us (25%)
  Pallas kernels  30.9 us (23%)
    ppermute x12, waiting for transfers between devices, along(): return lax.ppermute(array, ('c',) + EXPERT, pairs)  50.5 us
    ppermute x12, starting transfers between devices, along(): return lax.ppermute(array, ('c',) + EXPERT, pairs)  19.2 us
    ppermute x6, waiting for transfers between devices, moved(): lax.ppermute(array, axis, [(i, (i + step) % size) for i in range(size)])  14.6 us
    pallas_call x1, Pallas kernels, dispatch(): pl.pallas_call(dispatch_kernel, in_specs=[SCALARS, SCALARS, SCALARS, ANYW...  8.17 us
    ppermute x6, starting transfers between devices, moved(): lax.ppermute(array, axis, [(i, (i + step) % size) for i in range(size)])  6.81 us
    all_to_all x1, starting transfers between devices, exchanged(): return lax.all_to_all(array, axis, split_axis=0, concat_axis=0, tiled=True)  6.35 us
    pallas_call x1, Pallas kernels, mix_rows(): pl.pallas_call(mix_kernel, in_specs=[SCALARS, SCALARS, SCALARS, ANYWHERE,...  6.33 us
    pallas_call x1, Pallas kernels, fetch(): pl.pallas_call(fetch_kernel, in_specs=[ANYWHERE, ANYWHERE], out_specs=[WH...  5.93 us
  transfers between devices with their start and end apart: 24, of which 16 were waited for; matrix products, arithmetic and copies ran while one was open for 0% of the time, Pallas kernels for 13%

profile of v1, /device:TPU:0, one launch (start us, length us, event | category | flops | bytes accessed | tf_op | source)
XLA Modules:
  0.0 131.3 jit_solution(10631914445168319669)
XLA Ops:
  0.1 8.2 %dispatch.1 = (bf16[4,528,128]{2,1,0:T(8,128)(2,1)S(1)}, bf16[4,528,128]{2,1,0:T(8,128)(2,1)S(1)}, bf16[4,528,128]{2,1,0:T(8,128)(2,1)S(1)}, bf16[4,528,128]{2,1,0:T(8,128)(2,1)S(1)}) custom-call(s32[1,4]{1,0:T(1,128)} %lengths.3, s32[2,4]{1,0:T(2,128)} %bitcast.7, s32[4]{0:T(128)S(1)} %pad_add_fusion.place, bf16[1,4,512,1024]{3,2,1,0:T(8,128)(2,1)} %tokens.3, ...), custom_call_target="tpu_custom_call" | custom-call | tf_op jit(solution)/shard_map/dispatch/pallas_call | solution.py:189
  8.3 2.1 %collective-permute-start = (bf16[4,528,128]{2,1,0:T(8,128)(2,1)S(1)}, bf16[4,528,128]{2,1,0:T(8,128)(2,1)S(1)}, u32[]{:S(2)}, u32[]{:S(2)}) collective-permute-start(bf16[4,528,128]{2,1,0:T(8,128)(2,1)S(1)} %get-tuple-element.29), channel_id=1, source_target_pairs={{0,4},{1,5},{2,6},{3,7},{4,8},{5,9},{6,10},{7,11},{8,12},{9,13},{1... | collective-permute-start | bytes 1622024 | tf_op jit(solution)/shard_map/ppermute | solution.py:488
  10.4 3.6 %collective-permute-start.1 = (bf16[4,528,128]{2,1,0:T(8,128)(2,1)S(1)}, bf16[4,528,128]{2,1,0:T(8,128)(2,1)S(1)}, u32[]{:S(2)}, u32[]{:S(2)}) collective-permute-start(bf16[4,528,128]{2,1,0:T(8,128)(2,1)S(1)} %get-tuple-element.30), channel_id=1, source_target_pairs={{0,8},{1,9},{2,10},{3,11},{4,12},{5,13},{6,14},{7,15},{8,0},{9,1},... | collective-permute-start | bytes 1622024 | tf_op jit(solution)/shard_map/ppermute | solution.py:488
  14.0 1.0 collective-permute-start.2
  14.9 6.3 %mix_rows.1 = bf16[16,256,256]{2,1,0:T(8,128)(2,1)} custom-call(s32[1,4]{1,0:T(1,128)} %lengths.3, s32[2,4]{1,0:T(2,128)} %bitcast.8, s32[4]{0:T(128)S(1)} %pad_add_fusion.place, bf16[1,4,512,1024]{3,2,1,0:T(8,128)(2,1)} %tokens.3, bf16[1024,256]{1,0:T(8,128)(2,1)} %params.3), custom_call_target="tpu_custom_call" | custom-call | tf_op jit(solution)/shard_map/mix_rows/pallas_call | solution.py:167
  21.3 5.8 %collective-permute-done.1.refs_2_ = bf16[4,528,128]{2,1,0:T(8,128)(2,1)S(1)} collective-permute-done((bf16[4,528,128]{2,1,0:T(8,128)(2,1)S(1)}, bf16[4,528,128]{2,1,0:T(8,128)(2,1)S(1)}, u32[]{:S(2)}, u32[]{:S(2)}) %collective-permute-start.1) | collective-permute-done | bytes 540704 | tf_op jit(solution)/shard_map/ppermute | solution.py:488
  27.1 1.5 %merge.1 = (bf16[528,128]{1,0:T(8,128)(2,1)S(1)}, bf16[528,128]{1,0:T(8,128)(2,1)S(1)}, bf16[528,128]{1,0:T(8,128)(2,1)S(1)}, bf16[528,128]{1,0:T(8,128)(2,1)S(1)}) custom-call(s32[4]{0:T(128)S(1)} %pad_add_fusion.place, bf16[4,528,128]{2,1,0:T(8,128)(2,1)S(1)} %get-tuple-element.28.refs_0_, bf16[4,528,128]{2,1,0:T(8,128)(2,1)S(1)} %collective-permute-done.refs_1_, ...), custom_call_target="tpu_custom_call" | custom-call | tf_op jit(solution)/shard_map/merge/pallas_call | solution.py:249
  28.5 6.4 %all-to-all-start = ((bf16[16,256,256]{2,1,0:T(8,128)(2,1)}), bf16[16,256,256]{2,1,0:T(8,128)(2,1)S(1)}, u32[]{:S(2)}, u32[]{:S(2)}) async-start(bf16[16,256,256]{2,1,0:T(8,128)(2,1)} %mix_rows.1), calls=%async_computation | async-start | bytes 4194304 | tf_op jit(solution)/shard_map/all_to_all | solution.py:471
  34.9 1.9 %collective-permute-start.3 = (bf16[528,128]{1,0:T(8,128)(2,1)S(1)}, bf16[528,128]{1,0:T(8,128)(2,1)S(1)}, u32[]{:S(2)}, u32[]{:S(2)}) collective-permute-start(bf16[528,128]{1,0:T(8,128)(2,1)S(1)} %get-tuple-element.37), channel_id=1, source_target_pairs={{0,1},{1,2},{2,3},{3,0},{4,5},{5,6},{6,7},{7,4},{8,9},{9,10},{10,1... | collective-permute-start | bytes 405512 | tf_op jit(solution)/shard_map/ppermute | solution.py:488
  36.8 2.7 %collective-permute-start.4 = (bf16[528,128]{1,0:T(8,128)(2,1)S(1)}, bf16[528,128]{1,0:T(8,128)(2,1)S(1)}, u32[]{:S(2)}, u32[]{:S(2)}) collective-permute-start(bf16[528,128]{1,0:T(8,128)(2,1)S(1)} %get-tuple-element.38), channel_id=1, source_target_pairs={{0,2},{1,3},{2,0},{3,1},{4,6},{5,7},{6,4},{7,5},{8,10},{9,11},{10,... | collective-permute-start | bytes 405512 | tf_op jit(solution)/shard_map/ppermute | solution.py:488
  39.5 1.5 %collective-permute-start.5 = (bf16[528,128]{1,0:T(8,128)(2,1)S(1)}, bf16[528,128]{1,0:T(8,128)(2,1)S(1)}, u32[]{:S(2)}, u32[]{:S(2)}) collective-permute-start(bf16[528,128]{1,0:T(8,128)(2,1)S(1)} %get-tuple-element.39), channel_id=1, source_target_pairs={{0,3},{1,0},{2,1},{3,2},{4,7},{5,4},{6,5},{7,6},{8,11},{9,8},{10,9... | collective-permute-start | bytes 405512 | tf_op jit(solution)/shard_map/ppermute | solution.py:488
  41.0 20.1 %collective-permute-done.3.refs_1_ = bf16[528,128]{1,0:T(8,128)(2,1)S(1)} collective-permute-done((bf16[528,128]{1,0:T(8,128)(2,1)S(1)}, bf16[528,128]{1,0:T(8,128)(2,1)S(1)}, u32[]{:S(2)}, u32[]{:S(2)}) %collective-permute-start.3) | collective-permute-done | bytes 135200 | tf_op jit(solution)/shard_map/ppermute | solution.py:488
  61.1 5.1 %collective-permute-done.4.refs_2_ = bf16[528,128]{1,0:T(8,128)(2,1)S(1)} collective-permute-done((bf16[528,128]{1,0:T(8,128)(2,1)S(1)}, bf16[528,128]{1,0:T(8,128)(2,1)S(1)}, u32[]{:S(2)}, u32[]{:S(2)}) %collective-permute-start.4) | collective-permute-done | bytes 135200 | tf_op jit(solution)/shard_map/ppermute | solution.py:488
  66.2 0.6 own_slots.1
  66.7 3.1 %collective-permute-start.8 = (bf16[64,1024]{1,0:T(8,128)(2,1)S(1)}, bf16[64,1024]{1,0:T(8,128)(2,1)S(1)}, u32[]{:S(2)}, u32[]{:S(2)}) collective-permute-start(bf16[64,1024]{1,0:T(8,128)(2,1)S(1)} %get-tuple-element.42.refs_0_), channel_id=1, source_target_pairs={{0,96},{32,0},{64,32},{96,64},{1,97},{33,1},{65,33},{97,65},{2,98}... | collective-permute-start | bytes 393224 | tf_op jit(solution)/shard_map/ppermute | solution.py:476
  69.8 0.6 collective-permute-start.7
  70.4 1.0 collective-permute-start.6
  71.4 2.3 %collective-permute-done.8.refs_3_ = bf16[64,1024]{1,0:T(8,128)(2,1)S(1)} collective-permute-done((bf16[64,1024]{1,0:T(8,128)(2,1)S(1)}, bf16[64,1024]{1,0:T(8,128)(2,1)S(1)}, u32[]{:S(2)}, u32[]{:S(2)}) %collective-permute-start.8) | collective-permute-done | bytes 131104 | tf_op jit(solution)/shard_map/ppermute | solution.py:476
  73.7 2.6 %collective-permute-done.7.refs_2_ = bf16[64,1024]{1,0:T(8,128)(2,1)S(1)} collective-permute-done((bf16[64,1024]{1,0:T(8,128)(2,1)S(1)}, bf16[64,1024]{1,0:T(8,128)(2,1)S(1)}, u32[]{:S(2)}, u32[]{:S(2)}) %collective-permute-start.7) | collective-permute-done | bytes 131104 | tf_op jit(solution)/shard_map/ppermute | solution.py:476
  76.4 1.3 collective-permute-done.6.refs_1_
  77.7 5.9 %fetch.1 = (bf16[8,1024,512]{2,1,0:T(8,128)(2,1)S(1)}, bf16[8,512,1024]{2,1,0:T(8,128)(2,1)S(1)}) custom-call(bf16[8,1024,512]{2,1,0:T(8,128)(2,1)} %first.1, bf16[8,512,1024]{2,1,0:T(8,128)(2,1)} %second.1), custom_call_target="tpu_custom_call" | custom-call | tf_op jit(solution)/shard_map/fetch/pallas_call | solution.py:327
  83.7 3.8 %experts.1 = (f32[4,64,1024]{2,1,0:T(8,128)S(1)}, bf16[4,64,1024]{2,1,0:T(8,128)(2,1)S(1)}) custom-call(bf16[64,1024]{1,0:T(8,128)(2,1)S(1)} %get-tuple-element.42.refs_0_, bf16[64,1024]{1,0:T(8,128)(2,1)S(1)} %collective-permute-done.6.refs_1_, bf16[64,1024]{1,0:T(8,128)(2,1)S(1)} %collective-permute-done.7.refs_2_, ...), custom_call_target="tpu_custom_call" | custom-call | tf_op jit(solution)/shard_map/experts/pallas_call | solution.py:358
  87.5 0.6 collective-permute-start.13
  88.1 1.5 %collective-permute-done.13.other = bf16[4,64,1024]{2,1,0:T(8,128)(2,1)S(1)} collective-permute-done((bf16[4,64,1024]{2,1,0:T(8,128)(2,1)S(1)}, bf16[4,64,1024]{2,1,0:T(8,128)(2,1)S(1)}, u32[]{:S(2)}, u32[]{:S(2)}) %collective-permute-start.13) | collective-permute-done | bytes 524320 | tf_op jit(solution)/shard_map/ppermute | solution.py:467
  89.6 0.1 join.1
  89.7 0.6 collective-permute-start.14
  90.3 0.6 collective-permute-start.15
  91.0 0.9 collective-permute-start.16
  91.8 4.3 %collective-permute-done.14.refs_0_ = bf16[64,1024]{1,0:T(8,128)(2,1)S(1)} collective-permute-done((bf16[64,1024]{1,0:T(8,128)(2,1)S(1)}, bf16[64,1024]{1,0:T(8,128)(2,1)S(1)}, u32[]{:S(2)}, u32[]{:S(2)}) %collective-permute-start.14) | collective-permute-done | bytes 131104 | tf_op jit(solution)/shard_map/ppermute | solution.py:476
  96.1 2.1 %collective-permute-done.15.refs_1_ = bf16[64,1024]{1,0:T(8,128)(2,1)S(1)} collective-permute-done((bf16[64,1024]{1,0:T(8,128)(2,1)S(1)}, bf16[64,1024]{1,0:T(8,128)(2,1)S(1)}, u32[]{:S(2)}, u32[]{:S(2)}) %collective-permute-start.15) | collective-permute-done | bytes 131104 | tf_op jit(solution)/shard_map/ppermute | solution.py:476
  98.2 1.9 %collective-permute-done.16.refs_2_ = bf16[64,1024]{1,0:T(8,128)(2,1)S(1)} collective-permute-done((bf16[64,1024]{1,0:T(8,128)(2,1)S(1)}, bf16[64,1024]{1,0:T(8,128)(2,1)S(1)}, u32[]{:S(2)}, u32[]{:S(2)}) %collective-permute-start.16) | collective-permute-done | bytes 131104 | tf_op jit(solution)/shard_map/ppermute | solution.py:476
  100.2 0.2 collect.1.refs_0_
  100.4 2.0 %collective-permute-start.19 = (bf16[64,1024]{1,0:T(8,128)(2,1)S(1)}, bf16[64,1024]{1,0:T(8,128)(2,1)S(1)}, u32[]{:S(2)}, u32[]{:S(2)}) collective-permute-start(bf16[64,1024]{1,0:T(8,128)(2,1)S(1)} %collect.1.refs_0_), channel_id=1, source_target_pairs={{0,12},{1,13},{2,14},{3,15},{4,0},{5,1},{6,2},{7,3},{8,4},{9,5},{1... | collective-permute-start | bytes 393224 | tf_op jit(solution)/shard_map/ppermute | solution.py:488
  102.4 1.0 collective-permute-start.18
  103.4 1.3 %collective-permute-start.17 = (bf16[64,1024]{1,0:T(8,128)(2,1)S(1)}, bf16[64,1024]{1,0:T(8,128)(2,1)S(1)}, u32[]{:S(2)}, u32[]{:S(2)}) collective-permute-start(bf16[64,1024]{1,0:T(8,128)(2,1)S(1)} %collect.1.refs_0_), channel_id=1, source_target_pairs={{0,4},{1,5},{2,6},{3,7},{4,8},{5,9},{6,10},{7,11},{8,12},{9,13},{1... | collective-permute-start | bytes 393224 | tf_op jit(solution)/shard_map/ppermute | solution.py:488
  104.8 0.1 select_n.78
  104.9 0.5 collective-permute-done.19.refs_3_
  105.4 3.6 %collective-permute-done.18.refs_2_ = bf16[64,1024]{1,0:T(8,128)(2,1)S(1)} collective-permute-done((bf16[64,1024]{1,0:T(8,128)(2,1)S(1)}, bf16[64,1024]{1,0:T(8,128)(2,1)S(1)}, u32[]{:S(2)}, u32[]{:S(2)}) %collective-permute-start.18) | collective-permute-done | bytes 131104 | tf_op jit(solution)/shard_map/ppermute | solution.py:488
  109.0 1.3 %collective-permute-done.17.refs_1_ = bf16[64,1024]{1,0:T(8,128)(2,1)S(1)} collective-permute-done((bf16[64,1024]{1,0:T(8,128)(2,1)S(1)}, bf16[64,1024]{1,0:T(8,128)(2,1)S(1)}, u32[]{:S(2)}, u32[]{:S(2)}) %collective-permute-start.17) | collective-permute-done | bytes 131104 | tf_op jit(solution)/shard_map/ppermute | solution.py:488
  110.3 0.6 stack.21.refs_0_
  111.0 1.7 %collective-permute-start.21 = (bf16[4,64,1024]{2,1,0:T(8,128)(2,1)S(1)}, bf16[4,64,1024]{2,1,0:T(8,128)(2,1)}, u32[]{:S(2)}, u32[]{:S(2)}) collective-permute-start(bf16[4,64,1024]{2,1,0:T(8,128)(2,1)S(1)} %stack.21.refs_0_), channel_id=1, source_target_pairs={{0,2},{1,3},{2,0},{3,1},{4,6},{5,7},{6,4},{7,5},{8,10},{9,11},{10,... | collective-permute-start | bytes 1572872 | tf_op jit(solution)/shard_map/ppermute | solution.py:488
  112.7 0.3 collective-permute-start.20
  113.1 0.1 reshape.125
  113.2 0.1 select_reduce_fusion
  113.3 6.8 %collective-permute-done.22.refs_3_ = bf16[4,64,1024]{2,1,0:T(8,128)(2,1)S(1)} collective-permute-done((bf16[4,64,1024]{2,1,0:T(8,128)(2,1)S(1)}, bf16[4,64,1024]{2,1,0:T(8,128)(2,1)S(1)}, u32[]{:S(2)}, u32[]{:S(2)}) %collective-permute-start.22) | collective-permute-done | bytes 524320 | tf_op jit(solution)/shard_map/ppermute | solution.py:488
  120.1 1.8 %collective-permute-done.21.refs_2_ = bf16[4,64,1024]{2,1,0:T(8,128)(2,1)} collective-permute-done((bf16[4,64,1024]{2,1,0:T(8,128)(2,1)S(1)}, bf16[4,64,1024]{2,1,0:T(8,128)(2,1)}, u32[]{:S(2)}, u32[]{:S(2)}) %collective-permute-start.21) | collective-permute-done | bytes 524320 | tf_op jit(solution)/shard_map/ppermute | solution.py:488
  121.9 5.5 %collective-permute-done.20.refs_1_ = bf16[4,64,1024]{2,1,0:T(8,128)(2,1)} collective-permute-done((bf16[4,64,1024]{2,1,0:T(8,128)(2,1)S(1)}, bf16[4,64,1024]{2,1,0:T(8,128)(2,1)}, u32[]{:S(2)}, u32[]{:S(2)}) %collective-permute-start.20) | collective-permute-done | bytes 524320 | tf_op jit(solution)/shard_map/ppermute | solution.py:488
  127.5 3.7 %combine.1 = bf16[1,8,256,1024]{3,2,1,0:T(8,128)(2,1)} custom-call(s32[8]{0:T(128)S(1)} %get-tuple-element.52.source, s32[8]{0:T(128)S(1)} %get-tuple-element.51.seq, s32[4]{0:T(128)S(1)} %pad_add_fusion.place, bf16[16,256,256]{2,1,0:T(8,128)(2,1)S(1)} %all-to-all-done.mix, bf16[4,64,1024]{2,1,0:T(8,128)(2,1)S(1)} %stack.21.refs_0_, ...), custom_call_target="tpu_custom_call" | custom-call | tf_op jit(solution)/shard_map/combine/pallas_call | solution.py:451
  (19 shorter events, 0.4 us)
Async XLA Ops:
  8.3 13.0 %collective-permute-start = (bf16[4,528,128]{2,1,0:T(8,128)(2,1)S(1)}, bf16[4,528,128]{2,1,0:T(8,128)(2,1)S(1)}, u32[]{:S(2)}, u32[]{:S(2)}) collective-permute-start(bf16[4,528,128]{2,1,0:T(8,128)(2,1)S(1)} %get-tuple-element.29), channel_id=1, source_target_pairs={{0,4},{1,5},{2,6},{3,7},{4,8},{5,9},{6,10},{7,11},{8,12},{9,13},{1... | collective-permute-start | bytes 1622024 | tf_op jit(solution)/shard_map/ppermute | solution.py:488
  10.4 16.7 %collective-permute-start.1 = (bf16[4,528,128]{2,1,0:T(8,128)(2,1)S(1)}, bf16[4,528,128]{2,1,0:T(8,128)(2,1)S(1)}, u32[]{:S(2)}, u32[]{:S(2)}) collective-permute-start(bf16[4,528,128]{2,1,0:T(8,128)(2,1)S(1)} %get-tuple-element.30), channel_id=1, source_target_pairs={{0,8},{1,9},{2,10},{3,11},{4,12},{5,13},{6,14},{7,15},{8,0},{9,1},... | collective-permute-start | bytes 1622024 | tf_op jit(solution)/shard_map/ppermute | solution.py:488
  14.0 13.1 %collective-permute-start.2 = (bf16[4,528,128]{2,1,0:T(8,128)(2,1)S(1)}, bf16[4,528,128]{2,1,0:T(8,128)(2,1)S(1)}, u32[]{:S(2)}, u32[]{:S(2)}) collective-permute-start(bf16[4,528,128]{2,1,0:T(8,128)(2,1)S(1)} %get-tuple-element.31), channel_id=1, source_target_pairs={{0,12},{1,13},{2,14},{3,15},{4,0},{5,1},{6,2},{7,3},{8,4},{9,5},{1... | collective-permute-start | bytes 1622024 | tf_op jit(solution)/shard_map/ppermute | solution.py:488
  28.5 98.9 %all-to-all-start = ((bf16[16,256,256]{2,1,0:T(8,128)(2,1)}), bf16[16,256,256]{2,1,0:T(8,128)(2,1)S(1)}, u32[]{:S(2)}, u32[]{:S(2)}) async-start(bf16[16,256,256]{2,1,0:T(8,128)(2,1)} %mix_rows.1), calls=%async_computation | async-start | bytes 4194304 | tf_op jit(solution)/shard_map/all_to_all | solution.py:471
  34.9 26.2 %collective-permute-start.3 = (bf16[528,128]{1,0:T(8,128)(2,1)S(1)}, bf16[528,128]{1,0:T(8,128)(2,1)S(1)}, u32[]{:S(2)}, u32[]{:S(2)}) collective-permute-start(bf16[528,128]{1,0:T(8,128)(2,1)S(1)} %get-tuple-element.37), channel_id=1, source_target_pairs={{0,1},{1,2},{2,3},{3,0},{4,5},{5,6},{6,7},{7,4},{8,9},{9,10},{10,1... | collective-permute-start | bytes 405512 | tf_op jit(solution)/shard_map/ppermute | solution.py:488
  36.8 29.3 %collective-permute-start.4 = (bf16[528,128]{1,0:T(8,128)(2,1)S(1)}, bf16[528,128]{1,0:T(8,128)(2,1)S(1)}, u32[]{:S(2)}, u32[]{:S(2)}) collective-permute-start(bf16[528,128]{1,0:T(8,128)(2,1)S(1)} %get-tuple-element.38), channel_id=1, source_target_pairs={{0,2},{1,3},{2,0},{3,1},{4,6},{5,7},{6,4},{7,5},{8,10},{9,11},{10,... | collective-permute-start | bytes 405512 | tf_op jit(solution)/shard_map/ppermute | solution.py:488
  39.5 26.7 %collective-permute-start.5 = (bf16[528,128]{1,0:T(8,128)(2,1)S(1)}, bf16[528,128]{1,0:T(8,128)(2,1)S(1)}, u32[]{:S(2)}, u32[]{:S(2)}) collective-permute-start(bf16[528,128]{1,0:T(8,128)(2,1)S(1)} %get-tuple-element.39), channel_id=1, source_target_pairs={{0,3},{1,0},{2,1},{3,2},{4,7},{5,4},{6,5},{7,6},{8,11},{9,8},{10,9... | collective-permute-start | bytes 405512 | tf_op jit(solution)/shard_map/ppermute | solution.py:488
  66.7 7.0 %collective-permute-start.8 = (bf16[64,1024]{1,0:T(8,128)(2,1)S(1)}, bf16[64,1024]{1,0:T(8,128)(2,1)S(1)}, u32[]{:S(2)}, u32[]{:S(2)}) collective-permute-start(bf16[64,1024]{1,0:T(8,128)(2,1)S(1)} %get-tuple-element.42.refs_0_), channel_id=1, source_target_pairs={{0,96},{32,0},{64,32},{96,64},{1,97},{33,1},{65,33},{97,65},{2,98}... | collective-permute-start | bytes 393224 | tf_op jit(solution)/shard_map/ppermute | solution.py:476
  69.8 6.6 %collective-permute-start.7 = (bf16[64,1024]{1,0:T(8,128)(2,1)S(1)}, bf16[64,1024]{1,0:T(8,128)(2,1)S(1)}, u32[]{:S(2)}, u32[]{:S(2)}) collective-permute-start(bf16[64,1024]{1,0:T(8,128)(2,1)S(1)} %get-tuple-element.42.refs_0_), channel_id=1, source_target_pairs={{0,64},{32,96},{64,0},{96,32},{1,65},{33,97},{65,1},{97,33},{2,66}... | collective-permute-start | bytes 393224 | tf_op jit(solution)/shard_map/ppermute | solution.py:476
  70.4 7.2 %collective-permute-start.6 = (bf16[64,1024]{1,0:T(8,128)(2,1)S(1)}, bf16[64,1024]{1,0:T(8,128)(2,1)S(1)}, u32[]{:S(2)}, u32[]{:S(2)}) collective-permute-start(bf16[64,1024]{1,0:T(8,128)(2,1)S(1)} %get-tuple-element.42.refs_0_), channel_id=1, source_target_pairs={{0,32},{32,64},{64,96},{96,0},{1,33},{33,65},{65,97},{97,1},{2,34}... | collective-permute-start | bytes 393224 | tf_op jit(solution)/shard_map/ppermute | solution.py:476
  71.4 12.2 %collective-permute-start.9 = (bf16[64,1024]{1,0:T(8,128)(2,1)S(1)}, bf16[64,1024]{1,0:T(8,128)(2,1)S(1)}, u32[]{:S(2)}, u32[]{:S(2)}) collective-permute-start(bf16[64,1024]{1,0:T(8,128)(2,1)S(1)} %get-tuple-element.42.refs_0_), channel_id=1, source_target_pairs={{0,16},{16,0},{1,17},{17,1},{2,18},{18,2},{3,19},{19,3},{4,20},{20... | collective-permute-start | bytes 393224 | tf_op jit(solution)/shard_map/ppermute | solution.py:467
  73.7 9.9 %collective-permute-start.12 = (bf16[64,1024]{1,0:T(8,128)(2,1)S(1)}, bf16[64,1024]{1,0:T(8,128)(2,1)S(1)}, u32[]{:S(2)}, u32[]{:S(2)}) collective-permute-start(bf16[64,1024]{1,0:T(8,128)(2,1)S(1)} %collective-permute-done.8.refs_3_), channel_id=1, source_target_pairs={{0,16},{16,0},{1,17},{17,1},{2,18},{18,2},{3,19},{19,3},{4,20},{20... | collective-permute-start | bytes 393224 | tf_op jit(solution)/shard_map/ppermute | solution.py:467
  76.4 7.3 %collective-permute-start.11 = (bf16[64,1024]{1,0:T(8,128)(2,1)S(1)}, bf16[64,1024]{1,0:T(8,128)(2,1)S(1)}, u32[]{:S(2)}, u32[]{:S(2)}) collective-permute-start(bf16[64,1024]{1,0:T(8,128)(2,1)S(1)} %collective-permute-done.7.refs_2_), channel_id=1, source_target_pairs={{0,16},{16,0},{1,17},{17,1},{2,18},{18,2},{3,19},{19,3},{4,20},{20... | collective-permute-start | bytes 393224 | tf_op jit(solution)/shard_map/ppermute | solution.py:467
  77.7 6.0 %collective-permute-start.10 = (bf16[64,1024]{1,0:T(8,128)(2,1)S(1)}, bf16[64,1024]{1,0:T(8,128)(2,1)S(1)}, u32[]{:S(2)}, u32[]{:S(2)}) collective-permute-start(bf16[64,1024]{1,0:T(8,128)(2,1)S(1)} %collective-permute-done.6.refs_1_), channel_id=1, source_target_pairs={{0,16},{16,0},{1,17},{17,1},{2,18},{18,2},{3,19},{19,3},{4,20},{20... | collective-permute-start | bytes 393224 | tf_op jit(solution)/shard_map/ppermute | solution.py:467
  87.5 2.1 %collective-permute-start.13 = (bf16[4,64,1024]{2,1,0:T(8,128)(2,1)S(1)}, bf16[4,64,1024]{2,1,0:T(8,128)(2,1)S(1)}, u32[]{:S(2)}, u32[]{:S(2)}) collective-permute-start(bf16[4,64,1024]{2,1,0:T(8,128)(2,1)S(1)} %get-tuple-element.46), channel_id=1, source_target_pairs={{0,16},{16,0},{1,17},{17,1},{2,18},{18,2},{3,19},{19,3},{4,20},{20... | collective-permute-start | bytes 1572872 | tf_op jit(solution)/shard_map/ppermute | solution.py:467
  89.7 6.4 %collective-permute-start.14 = (bf16[64,1024]{1,0:T(8,128)(2,1)S(1)}, bf16[64,1024]{1,0:T(8,128)(2,1)S(1)}, u32[]{:S(2)}, u32[]{:S(2)}) collective-permute-start(bf16[64,1024]{1,0:T(8,128)(2,1)S(1)} %get-tuple-element.48), channel_id=1, source_target_pairs={{0,96},{32,0},{64,32},{96,64},{1,97},{33,1},{65,33},{97,65},{2,98}... | collective-permute-start | bytes 393224 | tf_op jit(solution)/shard_map/ppermute | solution.py:476
  90.3 7.9 %collective-permute-start.15 = (bf16[64,1024]{1,0:T(8,128)(2,1)S(1)}, bf16[64,1024]{1,0:T(8,128)(2,1)S(1)}, u32[]{:S(2)}, u32[]{:S(2)}) collective-permute-start(bf16[64,1024]{1,0:T(8,128)(2,1)S(1)} %get-tuple-element.49), channel_id=1, source_target_pairs={{0,64},{32,96},{64,0},{96,32},{1,65},{33,97},{65,1},{97,33},{2,66}... | collective-permute-start | bytes 393224 | tf_op jit(solution)/shard_map/ppermute | solution.py:476
  91.0 9.2 %collective-permute-start.16 = (bf16[64,1024]{1,0:T(8,128)(2,1)S(1)}, bf16[64,1024]{1,0:T(8,128)(2,1)S(1)}, u32[]{:S(2)}, u32[]{:S(2)}) collective-permute-start(bf16[64,1024]{1,0:T(8,128)(2,1)S(1)} %get-tuple-element.50), channel_id=1, source_target_pairs={{0,32},{32,64},{64,96},{96,0},{1,33},{33,65},{65,97},{97,1},{2,34}... | collective-permute-start | bytes 393224 | tf_op jit(solution)/shard_map/ppermute | solution.py:476
  100.4 5.0 %collective-permute-start.19 = (bf16[64,1024]{1,0:T(8,128)(2,1)S(1)}, bf16[64,1024]{1,0:T(8,128)(2,1)S(1)}, u32[]{:S(2)}, u32[]{:S(2)}) collective-permute-start(bf16[64,1024]{1,0:T(8,128)(2,1)S(1)} %collect.1.refs_0_), channel_id=1, source_target_pairs={{0,12},{1,13},{2,14},{3,15},{4,0},{5,1},{6,2},{7,3},{8,4},{9,5},{1... | collective-permute-start | bytes 393224 | tf_op jit(solution)/shard_map/ppermute | solution.py:488
  102.4 6.5 %collective-permute-start.18 = (bf16[64,1024]{1,0:T(8,128)(2,1)S(1)}, bf16[64,1024]{1,0:T(8,128)(2,1)S(1)}, u32[]{:S(2)}, u32[]{:S(2)}) collective-permute-start(bf16[64,1024]{1,0:T(8,128)(2,1)S(1)} %collect.1.refs_0_), channel_id=1, source_target_pairs={{0,8},{1,9},{2,10},{3,11},{4,12},{5,13},{6,14},{7,15},{8,0},{9,1},... | collective-permute-start | bytes 393224 | tf_op jit(solution)/shard_map/ppermute | solution.py:488
  103.4 6.9 %collective-permute-start.17 = (bf16[64,1024]{1,0:T(8,128)(2,1)S(1)}, bf16[64,1024]{1,0:T(8,128)(2,1)S(1)}, u32[]{:S(2)}, u32[]{:S(2)}) collective-permute-start(bf16[64,1024]{1,0:T(8,128)(2,1)S(1)} %collect.1.refs_0_), channel_id=1, source_target_pairs={{0,4},{1,5},{2,6},{3,7},{4,8},{5,9},{6,10},{7,11},{8,12},{9,13},{1... | collective-permute-start | bytes 393224 | tf_op jit(solution)/shard_map/ppermute | solution.py:488
  110.9 9.2 %collective-permute-start.22 = (bf16[4,64,1024]{2,1,0:T(8,128)(2,1)S(1)}, bf16[4,64,1024]{2,1,0:T(8,128)(2,1)S(1)}, u32[]{:S(2)}, u32[]{:S(2)}) collective-permute-start(bf16[4,64,1024]{2,1,0:T(8,128)(2,1)S(1)} %stack.21.refs_0_), channel_id=1, source_target_pairs={{0,3},{1,0},{2,1},{3,2},{4,7},{5,4},{6,5},{7,6},{8,11},{9,8},{10,9... | collective-permute-start | bytes 1572872 | tf_op jit(solution)/shard_map/ppermute | solution.py:488
  111.0 11.0 %collective-permute-start.21 = (bf16[4,64,1024]{2,1,0:T(8,128)(2,1)S(1)}, bf16[4,64,1024]{2,1,0:T(8,128)(2,1)}, u32[]{:S(2)}, u32[]{:S(2)}) collective-permute-start(bf16[4,64,1024]{2,1,0:T(8,128)(2,1)S(1)} %stack.21.refs_0_), channel_id=1, source_target_pairs={{0,2},{1,3},{2,0},{3,1},{4,6},{5,7},{6,4},{7,5},{8,10},{9,11},{10,... | collective-permute-start | bytes 1572872 | tf_op jit(solution)/shard_map/ppermute | solution.py:488
  112.7 14.8 %collective-permute-start.20 = (bf16[4,64,1024]{2,1,0:T(8,128)(2,1)S(1)}, bf16[4,64,1024]{2,1,0:T(8,128)(2,1)}, u32[]{:S(2)}, u32[]{:S(2)}) collective-permute-start(bf16[4,64,1024]{2,1,0:T(8,128)(2,1)S(1)} %stack.21.refs_0_), channel_id=1, source_target_pairs={{0,1},{1,2},{2,3},{3,0},{4,5},{5,6},{6,7},{7,4},{8,9},{9,10},{10,1... | collective-permute-start | bytes 1572872 | tf_op jit(solution)/shard_map/ppermute | solution.py:488

commit v2 on v1

--- a/solution.py
+++ b/solution.py
@@ -214,7 +214,7 @@
     return top, mass, factors
 
 
-def merge_kernel(place, *refs):
+def merge_kernel(step, place, *refs):
     side = 4
     sources, results = refs[:side], refs[side:]
     rows = sources[0].shape[1]
@@ -223,8 +223,8 @@
     stat_rows = rows - owned
     slabs = stat_rows // (seqs * owned)
     lane = lax.broadcasted_iota(jnp.int32, (owned, LANES), 1)
-    for k, result in enumerate(results):
-        ahead = lax.rem(place[3] + k, side)
+    for result in results:
+        ahead = lax.rem(place[3] + step, side)
         raws = [source[ahead, stat_rows:, :].astype(F32) for source in sources]
         top, mass, factors = joined_stats(raws)
         stat = jnp.where(lane >= TAGS, sum(raws), 0.0)
@@ -244,16 +244,15 @@
                 result[start : start + owned, :] = total.astype(BF16)
 
 
-def merge(place, parts):
+def merge(place, parts, step):
     side, rows, _ = parts[0].shape
     return pl.pallas_call(
-        merge_kernel,
+        functools.partial(merge_kernel, step),
         in_specs=[SCALARS] + [WHOLE] * side,
-        out_specs=[WHOLE] * side,
-        out_shape=[pltpu.VMEM((rows, LANES), BF16)] * side,
+        out_specs=[WHOLE],
+        out_shape=[pltpu.VMEM((rows, LANES), BF16)],
         compiler_params=small(4),
-        name="merge",
-    )(place, *in_vmem(*parts))
+    )(place, *in_vmem(*parts))[0]
 
 
 def expert_order(seqs, experts, per_expert, back):
@@ -504,9 +503,11 @@
     parts = dispatch(tokens, slot_params, lengths, table, place, side)
     mixes = mix_rows(tokens, slot_params, lengths, table, place, side)
     parts = [parts[0]] + [along(parts[k], True, k) for k in steps]
-    parts = merge(place, parts)
-    mixes, *parts = lax.optimization_barrier((mixes, *parts))
-    received = [parts[0]] + [along(parts[k], False, k) for k in steps]
+    received = []
+    for k in (*steps, 0):
+        piece = merge(place, parts, k)
+        received.append(along(piece, False, k) if k else piece)
+    received = received[-1:] + received[:-1]
     arrived = exchanged(mixes, EXPERT)
     slot_in, tags = own_slots(received, seqs, experts, owned)
     weights = fetch(w_in, w_out)

time: 132 us -> 122 us (0.924)
  waiting for transfers between devices: 66.6 us -> 50.2 us
  starting transfers between devices: 33 us -> 37.1 us
  Pallas kernels: 30.9 us -> 33.8 us
    ppermute x12, waiting for transfers between devices: 50.5 us -> 36.5 us  [along(): return lax.ppermute(array, ('c',) + EXPERT, pairs)]
    ppermute x6, starting transfers between devices: 6.81 us -> 9.62 us  [moved(): lax.ppermute(array, axis, [(i, (i + step) % size) for i in range(size)])]
    ppermute x12, starting transfers between devices: 19.2 us -> 21.8 us  [along(): return lax.ppermute(array, ('c',) + EXPERT, pairs)]
    ppermute x6, waiting for transfers between devices: 14.6 us -> 12.1 us  [moved(): lax.ppermute(array, axis, [(i, (i + step) % size) for i in range(size)])]
    pallas_call x1 -> x4, Pallas kernels: 1.45 us -> 3.24 us  [merge(): pl.pallas_call(functools.partial(merge_kernel, step), in_specs=[SCALARS]...]
    all_to_all x1, starting transfers between devices: 6.35 us -> 4.93 us  [exchanged(): return lax.all_to_all(array, axis, split_axis=0, concat_axis=0, tiled=True)]
  transfers between devices with their start and end apart: 24 -> 24, of which waited for: 16 -> 16; matrix products, arithmetic and copies ran while one was open for 0% -> 0% of each run, Pallas kernels for 13% -> 17%
where the time goes in v2:
time: 122 us
  waiting for transfers between devices  50.2 us (41%)
  starting transfers between devices  37.1 us (30%)
  Pallas kernels  33.8 us (28%)
    ppermute x12, waiting for transfers between devices, along(): return lax.ppermute(array, ('c',) + EXPERT, pairs)  36.5 us
    ppermute x12, starting transfers between devices, along(): return lax.ppermute(array, ('c',) + EXPERT, pairs)  21.8 us
    ppermute x6, waiting for transfers between devices, moved(): lax.ppermute(array, axis, [(i, (i + step) % size) for i in range(size)])  12.1 us
    ppermute x6, starting transfers between devices, moved(): lax.ppermute(array, axis, [(i, (i + step) % size) for i in range(size)])  9.62 us
    pallas_call x1, Pallas kernels, dispatch(): pl.pallas_call(dispatch_kernel, in_specs=[SCALARS, SCALARS, SCALARS, ANYW...  8.98 us
    pallas_call x1, Pallas kernels, mix_rows(): pl.pallas_call(mix_kernel, in_specs=[SCALARS, SCALARS, SCALARS, ANYWHERE,...  6.33 us
    pallas_call x1, Pallas kernels, fetch(): pl.pallas_call(fetch_kernel, in_specs=[ANYWHERE, ANYWHERE], out_specs=[WH...  5.93 us
    all_to_all x1, starting transfers between devices, exchanged(): return lax.all_to_all(array, axis, split_axis=0, concat_axis=0, tiled=True)  4.93 us
  transfers between devices with their start and end apart: 24, of which 16 were waited for; matrix products, arithmetic and copies ran while one was open for 0% of the time, Pallas kernels for 17%

profile of v2, /device:TPU:0, one launch (start us, length us, event | category | flops | bytes accessed | tf_op | source)
XLA Modules:
  0.0 122.0 jit_solution(16792398644585620611)
XLA Ops:
  0.1 9.0 %dispatch.1 = (bf16[4,528,128]{2,1,0:T(8,128)(2,1)S(1)}, bf16[4,528,128]{2,1,0:T(8,128)(2,1)}, bf16[4,528,128]{2,1,0:T(8,128)(2,1)S(1)}, bf16[4,528,128]{2,1,0:T(8,128)(2,1)S(1)}) custom-call(s32[1,4]{1,0:T(1,128)} %lengths.3, s32[2,4]{1,0:T(2,128)} %bitcast.7, s32[4]{0:T(128)S(1)} %pad_add_fusion.place, bf16[1,4,512,1024]{3,2,1,0:T(8,128)(2,1)} %tokens.3, ...), custom_call_target="tpu_custom_call" | custom-call | tf_op jit(solution)/shard_map/dispatch/pallas_call | solution.py:189
  9.1 2.1 %collective-permute-start = (bf16[4,528,128]{2,1,0:T(8,128)(2,1)}, bf16[4,528,128]{2,1,0:T(8,128)(2,1)S(1)}, u32[]{:S(2)}, u32[]{:S(2)}) collective-permute-start(bf16[4,528,128]{2,1,0:T(8,128)(2,1)} %get-tuple-element.20), channel_id=1, source_target_pairs={{0,4},{1,5},{2,6},{3,7},{4,8},{5,9},{6,10},{7,11},{8,12},{9,13},{1... | collective-permute-start | bytes 1622024 | tf_op jit(solution)/shard_map/ppermute | solution.py:487
  11.2 3.6 %collective-permute-start.1 = (bf16[4,528,128]{2,1,0:T(8,128)(2,1)S(1)}, bf16[4,528,128]{2,1,0:T(8,128)(2,1)S(1)}, u32[]{:S(2)}, u32[]{:S(2)}) collective-permute-start(bf16[4,528,128]{2,1,0:T(8,128)(2,1)S(1)} %get-tuple-element.21), channel_id=1, source_target_pairs={{0,8},{1,9},{2,10},{3,11},{4,12},{5,13},{6,14},{7,15},{8,0},{9,1},... | collective-permute-start | bytes 1622024 | tf_op jit(solution)/shard_map/ppermute | solution.py:487
  14.8 1.0 collective-permute-start.2
  15.8 6.3 %mix_rows.1 = bf16[16,256,256]{2,1,0:T(8,128)(2,1)} custom-call(s32[1,4]{1,0:T(1,128)} %lengths.3, s32[2,4]{1,0:T(2,128)} %bitcast.8, s32[4]{0:T(128)S(1)} %pad_add_fusion.place, bf16[1,4,512,1024]{3,2,1,0:T(8,128)(2,1)} %tokens.3, bf16[1024,256]{1,0:T(8,128)(2,1)} %params.3), custom_call_target="tpu_custom_call" | custom-call | tf_op jit(solution)/shard_map/mix_rows/pallas_call | solution.py:167
  22.1 4.9 %all-to-all-start = ((bf16[16,256,256]{2,1,0:T(8,128)(2,1)}), bf16[16,256,256]{2,1,0:T(8,128)(2,1)}, u32[]{:S(2)}, u32[]{:S(2)}) async-start(bf16[16,256,256]{2,1,0:T(8,128)(2,1)} %mix_rows.1), calls=%async_computation | async-start | bytes 4194304 | tf_op jit(solution)/shard_map/all_to_all | solution.py:470
  27.0 1.0 collective-permute-done.1.refs_2_
  28.1 0.8 shard_map.67
  28.9 2.8 %collective-permute-start.5 = (bf16[528,128]{1,0:T(8,128)(2,1)S(1)}, bf16[528,128]{1,0:T(8,128)(2,1)S(1)}, u32[]{:S(2)}, u32[]{:S(2)}) collective-permute-start(bf16[528,128]{1,0:T(8,128)(2,1)S(1)} %shard_map.67), channel_id=1, source_target_pairs={{0,3},{1,0},{2,1},{3,2},{4,7},{5,4},{6,5},{7,6},{8,11},{9,8},{10,9... | collective-permute-start | bytes 405512 | tf_op jit(solution)/shard_map/ppermute | solution.py:487
  31.7 0.8 shard_map.66
  32.6 0.9 collective-permute-start.4
  33.4 0.8 shard_map.65
  34.3 1.0 collective-permute-start.3
  35.2 0.8 shard_map.64.refs_0_
  36.0 17.9 %collective-permute-done.5.refs_3_ = bf16[528,128]{1,0:T(8,128)(2,1)S(1)} collective-permute-done((bf16[528,128]{1,0:T(8,128)(2,1)S(1)}, bf16[528,128]{1,0:T(8,128)(2,1)S(1)}, u32[]{:S(2)}, u32[]{:S(2)}) %collective-permute-start.5) | collective-permute-done | bytes 135200 | tf_op jit(solution)/shard_map/ppermute | solution.py:487
  53.9 2.7 %collective-permute-done.4.refs_2_ = bf16[528,128]{1,0:T(8,128)(2,1)S(1)} collective-permute-done((bf16[528,128]{1,0:T(8,128)(2,1)S(1)}, bf16[528,128]{1,0:T(8,128)(2,1)S(1)}, u32[]{:S(2)}, u32[]{:S(2)}) %collective-permute-start.4) | collective-permute-done | bytes 135200 | tf_op jit(solution)/shard_map/ppermute | solution.py:487
  56.5 0.6 own_slots.1
  57.1 1.6 %collective-permute-start.6 = (bf16[64,1024]{1,0:T(8,128)(2,1)S(1)}, bf16[64,1024]{1,0:T(8,128)(2,1)S(1)}, u32[]{:S(2)}, u32[]{:S(2)}) collective-permute-start(bf16[64,1024]{1,0:T(8,128)(2,1)S(1)} %get-tuple-element.24.refs_0_), channel_id=1, source_target_pairs={{0,32},{32,64},{64,96},{96,0},{1,33},{33,65},{65,97},{97,1},{2,34}... | collective-permute-start | bytes 393224 | tf_op jit(solution)/shard_map/ppermute | solution.py:475
  58.7 2.9 %collective-permute-start.7 = (bf16[64,1024]{1,0:T(8,128)(2,1)S(1)}, bf16[64,1024]{1,0:T(8,128)(2,1)S(1)}, u32[]{:S(2)}, u32[]{:S(2)}) collective-permute-start(bf16[64,1024]{1,0:T(8,128)(2,1)S(1)} %get-tuple-element.24.refs_0_), channel_id=1, source_target_pairs={{0,64},{32,96},{64,0},{96,32},{1,65},{33,97},{65,1},{97,33},{2,66}... | collective-permute-start | bytes 393224 | tf_op jit(solution)/shard_map/ppermute | solution.py:475
  61.6 1.3 %collective-permute-start.8 = (bf16[64,1024]{1,0:T(8,128)(2,1)S(1)}, bf16[64,1024]{1,0:T(8,128)(2,1)S(1)}, u32[]{:S(2)}, u32[]{:S(2)}) collective-permute-start(bf16[64,1024]{1,0:T(8,128)(2,1)S(1)} %get-tuple-element.24.refs_0_), channel_id=1, source_target_pairs={{0,96},{32,0},{64,32},{96,64},{1,97},{33,1},{65,33},{97,65},{2,98}... | collective-permute-start | bytes 393224 | tf_op jit(solution)/shard_map/ppermute | solution.py:475
  63.0 0.3 collective-permute-done.6.refs_1_
  63.5 2.5 %collective-permute-done.7.refs_2_ = bf16[64,1024]{1,0:T(8,128)(2,1)S(1)} collective-permute-done((bf16[64,1024]{1,0:T(8,128)(2,1)S(1)}, bf16[64,1024]{1,0:T(8,128)(2,1)S(1)}, u32[]{:S(2)}, u32[]{:S(2)}) %collective-permute-start.7) | collective-permute-done | bytes 131104 | tf_op jit(solution)/shard_map/ppermute | solution.py:475
  66.0 0.6 collective-permute-done.8.refs_3_
  66.6 5.9 %fetch.1 = (bf16[8,1024,512]{2,1,0:T(8,128)(2,1)S(1)}, bf16[8,512,1024]{2,1,0:T(8,128)(2,1)S(1)}) custom-call(bf16[8,1024,512]{2,1,0:T(8,128)(2,1)} %first.1, bf16[8,512,1024]{2,1,0:T(8,128)(2,1)} %second.1), custom_call_target="tpu_custom_call" | custom-call | tf_op jit(solution)/shard_map/fetch/pallas_call | solution.py:326
  72.6 3.8 %experts.1 = (f32[4,64,1024]{2,1,0:T(8,128)S(1)}, bf16[4,64,1024]{2,1,0:T(8,128)(2,1)S(1)}) custom-call(bf16[64,1024]{1,0:T(8,128)(2,1)S(1)} %get-tuple-element.24.refs_0_, bf16[64,1024]{1,0:T(8,128)(2,1)S(1)} %collective-permute-done.6.refs_1_, bf16[64,1024]{1,0:T(8,128)(2,1)S(1)} %collective-permute-done.7.refs_2_, ...), custom_call_target="tpu_custom_call" | custom-call | tf_op jit(solution)/shard_map/experts/pallas_call | solution.py:357
  76.4 0.6 collective-permute-start.13
  77.0 1.5 %collective-permute-done.13.other = bf16[4,64,1024]{2,1,0:T(8,128)(2,1)S(1)} collective-permute-done((bf16[4,64,1024]{2,1,0:T(8,128)(2,1)S(1)}, bf16[4,64,1024]{2,1,0:T(8,128)(2,1)S(1)}, u32[]{:S(2)}, u32[]{:S(2)}) %collective-permute-start.13) | collective-permute-done | bytes 524320 | tf_op jit(solution)/shard_map/ppermute | solution.py:466
  78.6 2.6 %collective-permute-start.14 = (bf16[64,1024]{1,0:T(8,128)(2,1)S(1)}, bf16[64,1024]{1,0:T(8,128)(2,1)S(1)}, u32[]{:S(2)}, u32[]{:S(2)}) collective-permute-start(bf16[64,1024]{1,0:T(8,128)(2,1)S(1)} %get-tuple-element.30), channel_id=1, source_target_pairs={{0,96},{32,0},{64,32},{96,64},{1,97},{33,1},{65,33},{97,65},{2,98}... | collective-permute-start | bytes 393224 | tf_op jit(solution)/shard_map/ppermute | solution.py:475
  81.3 0.5 collective-permute-start.15
  81.8 0.6 collective-permute-start.16
  82.4 5.0 %collective-permute-done.14.refs_0_ = bf16[64,1024]{1,0:T(8,128)(2,1)S(1)} collective-permute-done((bf16[64,1024]{1,0:T(8,128)(2,1)S(1)}, bf16[64,1024]{1,0:T(8,128)(2,1)S(1)}, u32[]{:S(2)}, u32[]{:S(2)}) %collective-permute-start.14) | collective-permute-done | bytes 131104 | tf_op jit(solution)/shard_map/ppermute | solution.py:475
  87.4 1.8 %collective-permute-done.15.refs_1_ = bf16[64,1024]{1,0:T(8,128)(2,1)S(1)} collective-permute-done((bf16[64,1024]{1,0:T(8,128)(2,1)S(1)}, bf16[64,1024]{1,0:T(8,128)(2,1)S(1)}, u32[]{:S(2)}, u32[]{:S(2)}) %collective-permute-start.15) | collective-permute-done | bytes 131104 | tf_op jit(solution)/shard_map/ppermute | solution.py:475
  89.2 1.8 %collective-permute-done.16.refs_2_ = bf16[64,1024]{1,0:T(8,128)(2,1)S(1)} collective-permute-done((bf16[64,1024]{1,0:T(8,128)(2,1)S(1)}, bf16[64,1024]{1,0:T(8,128)(2,1)S(1)}, u32[]{:S(2)}, u32[]{:S(2)}) %collective-permute-start.16) | collective-permute-done | bytes 131104 | tf_op jit(solution)/shard_map/ppermute | solution.py:475
  91.0 0.2 collect.1.refs_0_
  91.2 1.3 %collective-permute-start.17 = (bf16[64,1024]{1,0:T(8,128)(2,1)S(1)}, bf16[64,1024]{1,0:T(8,128)(2,1)S(1)}, u32[]{:S(2)}, u32[]{:S(2)}) collective-permute-start(bf16[64,1024]{1,0:T(8,128)(2,1)S(1)} %collect.1.refs_0_), channel_id=1, source_target_pairs={{0,4},{1,5},{2,6},{3,7},{4,8},{5,9},{6,10},{7,11},{8,12},{9,13},{1... | collective-permute-start | bytes 393224 | tf_op jit(solution)/shard_map/ppermute | solution.py:487
  92.5 2.7 %collective-permute-start.18 = (bf16[64,1024]{1,0:T(8,128)(2,1)S(1)}, bf16[64,1024]{1,0:T(8,128)(2,1)S(1)}, u32[]{:S(2)}, u32[]{:S(2)}) collective-permute-start(bf16[64,1024]{1,0:T(8,128)(2,1)S(1)} %collect.1.refs_0_), channel_id=1, source_target_pairs={{0,8},{1,9},{2,10},{3,11},{4,12},{5,13},{6,14},{7,15},{8,0},{9,1},... | collective-permute-start | bytes 393224 | tf_op jit(solution)/shard_map/ppermute | solution.py:487
  95.2 1.8 %collective-permute-start.19 = (bf16[64,1024]{1,0:T(8,128)(2,1)S(1)}, bf16[64,1024]{1,0:T(8,128)(2,1)S(1)}, u32[]{:S(2)}, u32[]{:S(2)}) collective-permute-start(bf16[64,1024]{1,0:T(8,128)(2,1)S(1)} %collect.1.refs_0_), channel_id=1, source_target_pairs={{0,12},{1,13},{2,14},{3,15},{4,0},{5,1},{6,2},{7,3},{8,4},{9,5},{1... | collective-permute-start | bytes 393224 | tf_op jit(solution)/shard_map/ppermute | solution.py:487
  97.2 0.3 collective-permute-done.17.refs_1_
  97.5 2.0 %collective-permute-done.18.refs_2_ = bf16[64,1024]{1,0:T(8,128)(2,1)S(1)} collective-permute-done((bf16[64,1024]{1,0:T(8,128)(2,1)S(1)}, bf16[64,1024]{1,0:T(8,128)(2,1)S(1)}, u32[]{:S(2)}, u32[]{:S(2)}) %collective-permute-start.18) | collective-permute-done | bytes 131104 | tf_op jit(solution)/shard_map/ppermute | solution.py:487
  99.5 0.6 collective-permute-done.19.refs_3_
  100.2 0.6 stack.21.refs_0_
  100.7 0.8 collective-permute-start.20
  101.6 2.6 %collective-permute-start.21 = (bf16[4,64,1024]{2,1,0:T(8,128)(2,1)S(1)}, bf16[4,64,1024]{2,1,0:T(8,128)(2,1)S(1)}, u32[]{:S(2)}, u32[]{:S(2)}) collective-permute-start(bf16[4,64,1024]{2,1,0:T(8,128)(2,1)S(1)} %stack.21.refs_0_), channel_id=1, source_target_pairs={{0,2},{1,3},{2,0},{3,1},{4,6},{5,7},{6,4},{7,5},{8,10},{9,11},{10,... | collective-permute-start | bytes 1572872 | tf_op jit(solution)/shard_map/ppermute | solution.py:487
  104.2 1.2 collective-permute-start.22
  105.7 5.5 %collective-permute-done.20.refs_1_ = bf16[4,64,1024]{2,1,0:T(8,128)(2,1)S(1)} collective-permute-done((bf16[4,64,1024]{2,1,0:T(8,128)(2,1)S(1)}, bf16[4,64,1024]{2,1,0:T(8,128)(2,1)S(1)}, u32[]{:S(2)}, u32[]{:S(2)}) %collective-permute-start.20) | collective-permute-done | bytes 524320 | tf_op jit(solution)/shard_map/ppermute | solution.py:487
  111.2 5.7 %collective-permute-done.21.refs_2_ = bf16[4,64,1024]{2,1,0:T(8,128)(2,1)S(1)} collective-permute-done((bf16[4,64,1024]{2,1,0:T(8,128)(2,1)S(1)}, bf16[4,64,1024]{2,1,0:T(8,128)(2,1)S(1)}, u32[]{:S(2)}, u32[]{:S(2)}) %collective-permute-start.21) | collective-permute-done | bytes 524320 | tf_op jit(solution)/shard_map/ppermute | solution.py:487
  117.0 0.8 collective-permute-done.22.refs_3_
  117.7 4.1 %combine.1 = bf16[1,8,256,1024]{3,2,1,0:T(8,128)(2,1)} custom-call(s32[8]{0:T(128)S(1)} %get-tuple-element.34.source, s32[8]{0:T(128)S(1)} %get-tuple-element.33.seq, s32[4]{0:T(128)S(1)} %pad_add_fusion.place, bf16[16,256,256]{2,1,0:T(8,128)(2,1)} %all-to-all-done.mix, bf16[4,64,1024]{2,1,0:T(8,128)(2,1)S(1)} %stack.21.refs_0_, ...), custom_call_target="tpu_custom_call" | custom-call | tf_op jit(solution)/shard_map/combine/pallas_call | solution.py:450
  (22 shorter events, 0.9 us)
Async XLA Ops:
  9.1 18.0 %collective-permute-start = (bf16[4,528,128]{2,1,0:T(8,128)(2,1)}, bf16[4,528,128]{2,1,0:T(8,128)(2,1)S(1)}, u32[]{:S(2)}, u32[]{:S(2)}) collective-permute-start(bf16[4,528,128]{2,1,0:T(8,128)(2,1)} %get-tuple-element.20), channel_id=1, source_target_pairs={{0,4},{1,5},{2,6},{3,7},{4,8},{5,9},{6,10},{7,11},{8,12},{9,13},{1... | collective-permute-start | bytes 1622024 | tf_op jit(solution)/shard_map/ppermute | solution.py:487
  11.2 16.9 %collective-permute-start.1 = (bf16[4,528,128]{2,1,0:T(8,128)(2,1)S(1)}, bf16[4,528,128]{2,1,0:T(8,128)(2,1)S(1)}, u32[]{:S(2)}, u32[]{:S(2)}) collective-permute-start(bf16[4,528,128]{2,1,0:T(8,128)(2,1)S(1)} %get-tuple-element.21), channel_id=1, source_target_pairs={{0,8},{1,9},{2,10},{3,11},{4,12},{5,13},{6,14},{7,15},{8,0},{9,1},... | collective-permute-start | bytes 1622024 | tf_op jit(solution)/shard_map/ppermute | solution.py:487
  14.8 13.3 %collective-permute-start.2 = (bf16[4,528,128]{2,1,0:T(8,128)(2,1)S(1)}, bf16[4,528,128]{2,1,0:T(8,128)(2,1)S(1)}, u32[]{:S(2)}, u32[]{:S(2)}) collective-permute-start(bf16[4,528,128]{2,1,0:T(8,128)(2,1)S(1)} %get-tuple-element.22), channel_id=1, source_target_pairs={{0,12},{1,13},{2,14},{3,15},{4,0},{5,1},{6,2},{7,3},{8,4},{9,5},{1... | collective-permute-start | bytes 1622024 | tf_op jit(solution)/shard_map/ppermute | solution.py:487
  22.1 83.6 %all-to-all-start = ((bf16[16,256,256]{2,1,0:T(8,128)(2,1)}), bf16[16,256,256]{2,1,0:T(8,128)(2,1)}, u32[]{:S(2)}, u32[]{:S(2)}) async-start(bf16[16,256,256]{2,1,0:T(8,128)(2,1)} %mix_rows.1), calls=%async_computation | async-start | bytes 4194304 | tf_op jit(solution)/shard_map/all_to_all | solution.py:470
  28.9 25.0 %collective-permute-start.5 = (bf16[528,128]{1,0:T(8,128)(2,1)S(1)}, bf16[528,128]{1,0:T(8,128)(2,1)S(1)}, u32[]{:S(2)}, u32[]{:S(2)}) collective-permute-start(bf16[528,128]{1,0:T(8,128)(2,1)S(1)} %shard_map.67), channel_id=1, source_target_pairs={{0,3},{1,0},{2,1},{3,2},{4,7},{5,4},{6,5},{7,6},{8,11},{9,8},{10,9... | collective-permute-start | bytes 405512 | tf_op jit(solution)/shard_map/ppermute | solution.py:487
  32.6 24.0 %collective-permute-start.4 = (bf16[528,128]{1,0:T(8,128)(2,1)S(1)}, bf16[528,128]{1,0:T(8,128)(2,1)S(1)}, u32[]{:S(2)}, u32[]{:S(2)}) collective-permute-start(bf16[528,128]{1,0:T(8,128)(2,1)S(1)} %shard_map.66), channel_id=1, source_target_pairs={{0,2},{1,3},{2,0},{3,1},{4,6},{5,7},{6,4},{7,5},{8,10},{9,11},{10,... | collective-permute-start | bytes 405512 | tf_op jit(solution)/shard_map/ppermute | solution.py:487
  34.3 22.3 %collective-permute-start.3 = (bf16[528,128]{1,0:T(8,128)(2,1)S(1)}, bf16[528,128]{1,0:T(8,128)(2,1)S(1)}, u32[]{:S(2)}, u32[]{:S(2)}) collective-permute-start(bf16[528,128]{1,0:T(8,128)(2,1)S(1)} %shard_map.65), channel_id=1, source_target_pairs={{0,1},{1,2},{2,3},{3,0},{4,5},{5,6},{6,7},{7,4},{8,9},{9,10},{10,1... | collective-permute-start | bytes 405512 | tf_op jit(solution)/shard_map/ppermute | solution.py:487
  57.1 6.2 %collective-permute-start.6 = (bf16[64,1024]{1,0:T(8,128)(2,1)S(1)}, bf16[64,1024]{1,0:T(8,128)(2,1)S(1)}, u32[]{:S(2)}, u32[]{:S(2)}) collective-permute-start(bf16[64,1024]{1,0:T(8,128)(2,1)S(1)} %get-tuple-element.24.refs_0_), channel_id=1, source_target_pairs={{0,32},{32,64},{64,96},{96,0},{1,33},{33,65},{65,97},{97,1},{2,34}... | collective-permute-start | bytes 393224 | tf_op jit(solution)/shard_map/ppermute | solution.py:475
  58.7 7.2 %collective-permute-start.7 = (bf16[64,1024]{1,0:T(8,128)(2,1)S(1)}, bf16[64,1024]{1,0:T(8,128)(2,1)S(1)}, u32[]{:S(2)}, u32[]{:S(2)}) collective-permute-start(bf16[64,1024]{1,0:T(8,128)(2,1)S(1)} %get-tuple-element.24.refs_0_), channel_id=1, source_target_pairs={{0,64},{32,96},{64,0},{96,32},{1,65},{33,97},{65,1},{97,33},{2,66}... | collective-permute-start | bytes 393224 | tf_op jit(solution)/shard_map/ppermute | solution.py:475
  61.6 5.0 %collective-permute-start.8 = (bf16[64,1024]{1,0:T(8,128)(2,1)S(1)}, bf16[64,1024]{1,0:T(8,128)(2,1)S(1)}, u32[]{:S(2)}, u32[]{:S(2)}) collective-permute-start(bf16[64,1024]{1,0:T(8,128)(2,1)S(1)} %get-tuple-element.24.refs_0_), channel_id=1, source_target_pairs={{0,96},{32,0},{64,32},{96,64},{1,97},{33,1},{65,33},{97,65},{2,98}... | collective-permute-start | bytes 393224 | tf_op jit(solution)/shard_map/ppermute | solution.py:475
  63.0 9.6 %collective-permute-start.9 = (bf16[64,1024]{1,0:T(8,128)(2,1)S(1)}, bf16[64,1024]{1,0:T(8,128)(2,1)S(1)}, u32[]{:S(2)}, u32[]{:S(2)}) collective-permute-start(bf16[64,1024]{1,0:T(8,128)(2,1)S(1)} %get-tuple-element.24.refs_0_), channel_id=1, source_target_pairs={{0,16},{16,0},{1,17},{17,1},{2,18},{18,2},{3,19},{19,3},{4,20},{20... | collective-permute-start | bytes 393224 | tf_op jit(solution)/shard_map/ppermute | solution.py:466
  63.3 9.2 %collective-permute-start.10 = (bf16[64,1024]{1,0:T(8,128)(2,1)S(1)}, bf16[64,1024]{1,0:T(8,128)(2,1)S(1)}, u32[]{:S(2)}, u32[]{:S(2)}) collective-permute-start(bf16[64,1024]{1,0:T(8,128)(2,1)S(1)} %collective-permute-done.6.refs_1_), channel_id=1, source_target_pairs={{0,16},{16,0},{1,17},{17,1},{2,18},{18,2},{3,19},{19,3},{4,20},{20... | collective-permute-start | bytes 393224 | tf_op jit(solution)/shard_map/ppermute | solution.py:466
  66.0 6.6 %collective-permute-start.11 = (bf16[64,1024]{1,0:T(8,128)(2,1)S(1)}, bf16[64,1024]{1,0:T(8,128)(2,1)S(1)}, u32[]{:S(2)}, u32[]{:S(2)}) collective-permute-start(bf16[64,1024]{1,0:T(8,128)(2,1)S(1)} %collective-permute-done.7.refs_2_), channel_id=1, source_target_pairs={{0,16},{16,0},{1,17},{17,1},{2,18},{18,2},{3,19},{19,3},{4,20},{20... | collective-permute-start | bytes 393224 | tf_op jit(solution)/shard_map/ppermute | solution.py:466
  66.6 6.0 %collective-permute-start.12 = (bf16[64,1024]{1,0:T(8,128)(2,1)S(1)}, bf16[64,1024]{1,0:T(8,128)(2,1)S(1)}, u32[]{:S(2)}, u32[]{:S(2)}) collective-permute-start(bf16[64,1024]{1,0:T(8,128)(2,1)S(1)} %collective-permute-done.8.refs_3_), channel_id=1, source_target_pairs={{0,16},{16,0},{1,17},{17,1},{2,18},{18,2},{3,19},{19,3},{4,20},{20... | collective-permute-start | bytes 393224 | tf_op jit(solution)/shard_map/ppermute | solution.py:466
  76.4 2.1 %collective-permute-start.13 = (bf16[4,64,1024]{2,1,0:T(8,128)(2,1)S(1)}, bf16[4,64,1024]{2,1,0:T(8,128)(2,1)S(1)}, u32[]{:S(2)}, u32[]{:S(2)}) collective-permute-start(bf16[4,64,1024]{2,1,0:T(8,128)(2,1)S(1)} %get-tuple-element.28), channel_id=1, source_target_pairs={{0,16},{16,0},{1,17},{17,1},{2,18},{18,2},{3,19},{19,3},{4,20},{20... | collective-permute-start | bytes 1572872 | tf_op jit(solution)/shard_map/ppermute | solution.py:466
  78.6 8.8 %collective-permute-start.14 = (bf16[64,1024]{1,0:T(8,128)(2,1)S(1)}, bf16[64,1024]{1,0:T(8,128)(2,1)S(1)}, u32[]{:S(2)}, u32[]{:S(2)}) collective-permute-start(bf16[64,1024]{1,0:T(8,128)(2,1)S(1)} %get-tuple-element.30), channel_id=1, source_target_pairs={{0,96},{32,0},{64,32},{96,64},{1,97},{33,1},{65,33},{97,65},{2,98}... | collective-permute-start | bytes 393224 | tf_op jit(solution)/shard_map/ppermute | solution.py:475
  81.3 7.9 %collective-permute-start.15 = (bf16[64,1024]{1,0:T(8,128)(2,1)S(1)}, bf16[64,1024]{1,0:T(8,128)(2,1)S(1)}, u32[]{:S(2)}, u32[]{:S(2)}) collective-permute-start(bf16[64,1024]{1,0:T(8,128)(2,1)S(1)} %get-tuple-element.31), channel_id=1, source_target_pairs={{0,64},{32,96},{64,0},{96,32},{1,65},{33,97},{65,1},{97,33},{2,66}... | collective-permute-start | bytes 393224 | tf_op jit(solution)/shard_map/ppermute | solution.py:475
  81.8 9.2 %collective-permute-start.16 = (bf16[64,1024]{1,0:T(8,128)(2,1)S(1)}, bf16[64,1024]{1,0:T(8,128)(2,1)S(1)}, u32[]{:S(2)}, u32[]{:S(2)}) collective-permute-start(bf16[64,1024]{1,0:T(8,128)(2,1)S(1)} %get-tuple-element.32), channel_id=1, source_target_pairs={{0,32},{32,64},{64,96},{96,0},{1,33},{33,65},{65,97},{97,1},{2,34}... | collective-permute-start | bytes 393224 | tf_op jit(solution)/shard_map/ppermute | solution.py:475
  91.2 6.2 %collective-permute-start.17 = (bf16[64,1024]{1,0:T(8,128)(2,1)S(1)}, bf16[64,1024]{1,0:T(8,128)(2,1)S(1)}, u32[]{:S(2)}, u32[]{:S(2)}) collective-permute-start(bf16[64,1024]{1,0:T(8,128)(2,1)S(1)} %collect.1.refs_0_), channel_id=1, source_target_pairs={{0,4},{1,5},{2,6},{3,7},{4,8},{5,9},{6,10},{7,11},{8,12},{9,13},{1... | collective-permute-start | bytes 393224 | tf_op jit(solution)/shard_map/ppermute | solution.py:487
  92.5 7.0 %collective-permute-start.18 = (bf16[64,1024]{1,0:T(8,128)(2,1)S(1)}, bf16[64,1024]{1,0:T(8,128)(2,1)S(1)}, u32[]{:S(2)}, u32[]{:S(2)}) collective-permute-start(bf16[64,1024]{1,0:T(8,128)(2,1)S(1)} %collect.1.refs_0_), channel_id=1, source_target_pairs={{0,8},{1,9},{2,10},{3,11},{4,12},{5,13},{6,14},{7,15},{8,0},{9,1},... | collective-permute-start | bytes 393224 | tf_op jit(solution)/shard_map/ppermute | solution.py:487
  95.2 5.0 %collective-permute-start.19 = (bf16[64,1024]{1,0:T(8,128)(2,1)S(1)}, bf16[64,1024]{1,0:T(8,128)(2,1)S(1)}, u32[]{:S(2)}, u32[]{:S(2)}) collective-permute-start(bf16[64,1024]{1,0:T(8,128)(2,1)S(1)} %collect.1.refs_0_), channel_id=1, source_target_pairs={{0,12},{1,13},{2,14},{3,15},{4,0},{5,1},{6,2},{7,3},{8,4},{9,5},{1... | collective-permute-start | bytes 393224 | tf_op jit(solution)/shard_map/ppermute | solution.py:487
  100.7 10.5 %collective-permute-start.20 = (bf16[4,64,1024]{2,1,0:T(8,128)(2,1)S(1)}, bf16[4,64,1024]{2,1,0:T(8,128)(2,1)S(1)}, u32[]{:S(2)}, u32[]{:S(2)}) collective-permute-start(bf16[4,64,1024]{2,1,0:T(8,128)(2,1)S(1)} %stack.21.refs_0_), channel_id=1, source_target_pairs={{0,1},{1,2},{2,3},{3,0},{4,5},{5,6},{6,7},{7,4},{8,9},{9,10},{10,1... | collective-permute-start | bytes 1572872 | tf_op jit(solution)/shard_map/ppermute | solution.py:487
  101.6 15.4 %collective-permute-start.21 = (bf16[4,64,1024]{2,1,0:T(8,128)(2,1)S(1)}, bf16[4,64,1024]{2,1,0:T(8,128)(2,1)S(1)}, u32[]{:S(2)}, u32[]{:S(2)}) collective-permute-start(bf16[4,64,1024]{2,1,0:T(8,128)(2,1)S(1)} %stack.21.refs_0_), channel_id=1, source_target_pairs={{0,2},{1,3},{2,0},{3,1},{4,6},{5,7},{6,4},{7,5},{8,10},{9,11},{10,... | collective-permute-start | bytes 1572872 | tf_op jit(solution)/shard_map/ppermute | solution.py:487
  104.2 13.5 %collective-permute-start.22 = (bf16[4,64,1024]{2,1,0:T(8,128)(2,1)S(1)}, bf16[4,64,1024]{2,1,0:T(8,128)(2,1)S(1)}, u32[]{:S(2)}, u32[]{:S(2)}) collective-permute-start(bf16[4,64,1024]{2,1,0:T(8,128)(2,1)S(1)} %stack.21.refs_0_), channel_id=1, source_target_pairs={{0,3},{1,0},{2,1},{3,2},{4,7},{5,4},{6,5},{7,6},{8,11},{9,8},{10,9... | collective-permute-start | bytes 1572872 | tf_op jit(solution)/shard_map/ppermute | solution.py:487
